TPU v7x, 32 devices: a whole 2x2x4 slice. The times are simulated.
32 devices in a mesh: grp: 4 (over z), wave: 8 (over y, x, core).
Axes of the slice: x: 2, y: 2, z: 4, core: 2. Of those that a mesh axis runs over, the one named last changes fastest.
Arguments:
- state: bfloat16 [275, 61760], P(None, ('grp', 'wave')), may hold values from -6 to 6
- held_orders: int32 [160], P(('grp', 'wave')), may hold values from -1 to 95, as said below
- pair_lows: int32 [96], P(('grp', 'wave')), may hold values from 0 to 95, each once
- inverses: bfloat16 [96, 2, 137, 137], P(('grp', 'wave')), may hold values from -2 to 3
- height_operator: bfloat16 [137, 137], replicated, may hold values from -0.5 to 0.5
- pressure_column: bfloat16 [137], replicated, may hold values from -5 to 5
- thermal_response_matrix: bfloat16 [137, 137], replicated, may hold values from -0.5 to 0.5
- mass_row: bfloat16 [137], replicated, may hold values from -0.5 to 0.5
Outputs:
- advanced: bfloat16 [275, 61760], P(None, ('grp', 'wave'))
Inputs may be any that keep to these rules, and one draw needn't show every extreme that they name: `held_orders`: each of 0 to 95 appears exactly once, all other entries are -1; some device has all 5 of its slots filled.
All inputs are finite; a program needn't handle non-finite values.
Results may differ from a plain program's by a relative error of at most 0.0052.
Values may be sent and summed in bfloat16 or wider, within the bound.
A program may use at most 128 MiB of HBM per device.

v0:
```python
import functools

import jax
import jax.numpy as jnp
from jax import lax
from jax.experimental import pallas as pl
from jax.experimental.pallas import tpu as pltpu
from jax.sharding import PartitionSpec as P

MESH = pl.DeviceIdType.MESH
LANES = 128
ROWS_TILE = 16
KEEP_BYTES = 24 << 20


def ceil_to(value, step):
    return -(-value // step) * step


def kernel(
    size,
    held,
    lows,
    state_far,
    inverses,
    height_operator,
    pressure_column,
    thermal_response,
    mass_row,
    out,
    state,
    info,
    matrices,
    rest,
    right,
    pick,
    outgoing,
    arrived,
    solved,
    returned,
    total,
    info_send,
    info_recv,
    z_send,
    z_recv,
    out_send,
    out_recv,
    back_send,
    back_recv,
    state_sem,
):
    Z, W, levels, slots, pairs = size
    half_count = Z * W * pairs
    truncation = 2 * half_count - 1
    slot_width = 2 * (truncation + 2)
    width = slots * slot_width
    denom = float(truncation * (truncation + 1))
    devices = Z * W
    per_pair = 4 * slots
    block_pairs = Z * pairs // 2
    first_extra = block_pairs * per_pair
    tail = levels - LANES
    chunks = pairs + 1
    keep = pick.shape[0] > 1
    z = lax.axis_index("grp")
    w = lax.axis_index("wave")
    me = z * W + w

    barrier = pltpu.get_barrier_semaphore()

    def greet(k, carry):
        other = lax.rem(me + k, devices)
        pl.semaphore_signal(
            barrier, inc=1, device_id=(other // W, lax.rem(other, W)), device_id_type=MESH
        )
        return carry

    lax.fori_loop(1, devices, greet, 0)
    fetch = pltpu.make_async_copy(state_far, state, state_sem)
    fetch.start()

    lane = lax.broadcasted_iota(jnp.int32, (1, LANES), 1)
    extra = lane >= first_extra
    used = lane < first_extra + slots
    lane_pair = lane // per_pair
    lane_member = lax.rem(lane, per_pair) // (2 * slots)
    lane_slot = jnp.where(extra, lane - first_extra, lax.rem(lane, 2 * slots) // 2)
    orders = jnp.full((1, LANES), -1, jnp.int32)
    for s in range(slots):
        orders = jnp.where(lane_slot == s, held[s], orders)
    row = lax.broadcasted_iota(jnp.int32, (pairs + 1, LANES), 0)
    tile = jnp.broadcast_to(orders, (pairs + 1, LANES))
    for j in range(pairs):
        tile = jnp.where(row == j, lows[j], tile)
    info[me] = tile

    ends = []
    for i in range(2 * pairs):
        matrices[z, i, 0:levels, :] = inverses[i]
        ends.append(inverses[i, :, LANES:levels].astype(jnp.float32))
    ends = jnp.concatenate(ends, axis=1).astype(jnp.bfloat16)
    rest[z, 0:levels, 0 : 2 * pairs * tail] = ends

    pl.semaphore_wait(barrier, devices - 1)

    def info_copy(k):
        other = lax.rem(me + k, devices)
        return pltpu.make_async_remote_copy(
            src_ref=info.at[me],
            dst_ref=info.at[me],
            send_sem=info_send.at[k],
            recv_sem=info_recv.at[k],
            device_id=(other // W, lax.rem(other, W)),
            device_id_type=MESH,
        )

    def info_arrival(k):
        source = lax.rem(me + devices - k, devices)
        return pltpu.make_async_remote_copy(
            src_ref=info.at[source],
            dst_ref=info.at[source],
            send_sem=info_send.at[k],
            recv_sem=info_recv.at[k],
            device_id=(source // W, lax.rem(source, W)),
            device_id_type=MESH,
        )

    def start_info(k, carry):
        info_copy(k).start()
        return carry

    lax.fori_loop(1, devices, start_info, 0)

    def z_copy(g, c, way):
        if c < pairs:
            ref = matrices.at[g, pl.ds(2 * c, 2), :, pl.ds(0, LANES)]
        else:
            ref = rest.at[g]
        step = 1 if way == 0 else -1
        return pltpu.make_async_remote_copy(
            src_ref=ref,
            dst_ref=ref,
            send_sem=z_send.at[g, c, way],
            recv_sem=z_recv.at[g, c],
            device_id=(z + step, w),
            device_id_type=MESH,
        )

    def forward(g, c):
        @pl.when(jnp.logical_and(g <= z, z < Z - 1))
        def _():
            z_copy(g, c, 0).start()

        @pl.when(jnp.logical_and(g >= z, z > 0))
        def _():
            z_copy(g, c, 1).start()

    def group_at(t):
        g = z
        for zz in range(Z):
            by_distance = sorted(range(Z), key=lambda a: abs(a - zz))
            g = jnp.where(z == zz, by_distance[t], g)
        return g

    def relay(t):
        g = group_at(t)
        for c in range(chunks):
            z_copy(g, c, 0).wait_recv()
            forward(g, c)

    for c in range(chunks):
        forward(z, c)

    column = lax.broadcasted_iota(jnp.int32, (1, width), 1)
    column_order = jnp.full((1, width), -1, jnp.int32)
    column_start = jnp.zeros((1, width), jnp.int32)
    for s in range(slots):
        inside = jnp.logical_and(column >= s * slot_width, column < (s + 1) * slot_width)
        column_order = jnp.where(inside, held[s], column_order)
        column_start = jnp.where(inside, s * slot_width, column_start)
    coefficient = (column - column_start) // 2
    degree = jnp.where(
        coefficient <= truncation - column_order, column_order + coefficient, coefficient - 1
    )
    lap_scale = (degree * (degree + 1)).astype(jnp.float32) / denom
    height = height_operator[...].astype(jnp.float32)
    pressure_row = jnp.broadcast_to(
        pressure_column[...].astype(jnp.float32).reshape(1, levels), height.shape
    )
    across = lax.broadcasted_iota(jnp.int32, height.shape, 1)
    down = lax.broadcasted_iota(jnp.int32, height.shape, 0)
    pressure_side = jnp.sum(
        jnp.where(across == down, pressure_row, 0.0), axis=1, keepdims=True
    )
    height = jnp.concatenate(
        [jnp.zeros((levels, tail), jnp.float32), height, pressure_side], axis=1
    ).astype(jnp.bfloat16)
    fetch.wait()
    drive = jnp.dot(height, state[LANES:, :], preferred_element_type=jnp.float32)
    right[0:levels, :] = (
        state[0:levels, :].astype(jnp.float32) + lap_scale * drive
    ).astype(jnp.bfloat16)

    def wait_info(k, carry):
        info_arrival(k).wait_recv()
        return carry

    lax.fori_loop(1, devices, wait_info, 0)

    def build(k, place):
        d = lax.rem(w + k, W)
        tables = [info[g * W + d] for g in range(Z)]
        low_rows = [tables[g][j : j + 1] for g in range(Z) for j in range(pairs)]
        hit = low_rows[0] == orders
        for low in low_rows[1:]:
            hit = jnp.logical_or(hit, low == orders)
        for b in range(2):
            low = jnp.zeros((1, LANES), jnp.int32)
            for p in range(block_pairs):
                low = jnp.where(lane_pair == p, low_rows[b * block_pairs + p], low)
            merged = jnp.where(orders <= low, low - orders, truncation + 1 - low)
            position = jnp.where(lane_member == 0, merged, truncation - low - orders)
            position = jnp.where(extra, truncation + 1 - orders, position)
            part = jnp.where(extra, b, lax.rem(lane, 2))
            target = lane_slot * slot_width + 2 * position + part
            target = jnp.where(jnp.logical_and(orders >= 0, used), target, -1)
            target = jnp.where(jnp.logical_and(extra, jnp.logical_not(hit)), -1, target)
            at = lax.broadcasted_iota(jnp.int32, (width, LANES), 0)
            pick[place, :, b * LANES : (b + 1) * LANES] = jnp.where(
                at == target, 1.0, 0.0
            ).astype(jnp.bfloat16)

    def place_of(k):
        return k if keep else 0

    def out_copy(k):
        return pltpu.make_async_remote_copy(
            src_ref=outgoing.at[k],
            dst_ref=arrived.at[k],
            send_sem=out_send.at[k],
            recv_sem=out_recv.at[k],
            device_id=(z, lax.rem(w + k, W)),
            device_id_type=MESH,
        )

    def back_copy(k):
        return pltpu.make_async_remote_copy(
            src_ref=solved.at[k],
            dst_ref=returned.at[k],
            send_sem=back_send.at[k],
            recv_sem=back_recv.at[k],
            device_id=(z, lax.rem(w + W - k, W)),
            device_id_type=MESH,
        )

    def message(k):
        build(k, place_of(k))
        return jnp.dot(
            right[...], pick[place_of(k)], preferred_element_type=jnp.float32
        ).astype(jnp.bfloat16)

    def send(k, carry):
        outgoing[k] = message(k)
        out_copy(k).start()
        return carry

    lax.fori_loop(1, W, send, 0)
    arrived[0] = message(0)

    for t in range(1, Z - 1):
        relay(t)

    def wait_out(k, carry):
        out_copy(k).wait_recv()
        return carry

    lax.fori_loop(1, W, wait_out, 0)

    wide_lane = jnp.concatenate([lane, lane], axis=1)
    wide_pair = wide_lane // per_pair
    wide_member = lax.rem(wide_lane, per_pair) // (2 * slots)
    wide_extra = jnp.logical_and(wide_lane >= first_extra, wide_lane < first_extra + slots)

    def solve(t):
        g = group_at(t)
        b = (g * pairs) // block_pairs
        for i in range(2 * pairs):
            if t > 0:
                piece = rest[g].astype(jnp.float32)[:, i * tail : (i + 1) * tail]
                matrices[g, i, :, LANES:levels] = piece.astype(jnp.bfloat16)
        near = pl.ds(pl.multiple_of(b * LANES, LANES), LANES)
        far = pl.ds(pl.multiple_of((1 - b) * LANES, LANES), LANES)
        mine = info[g * W + w]

        def two_sources(i, carry):
            k0, k1 = 2 * i, 2 * i + 1
            s0 = lax.rem(w + W - k0, W)
            s1 = lax.rem(w + W - k1, W)
            m0 = info[z * W + s0][pairs : pairs + 1]
            m1 = info[z * W + s1][pairs : pairs + 1]
            m = jnp.concatenate([m0, m1], axis=1)
            x_near = jnp.concatenate(
                [arrived[k0, 0:levels, near], arrived[k1, 0:levels, near]], axis=1
            )
            x_far = jnp.concatenate(
                [arrived[k0, 0:levels, far], arrived[k1, 0:levels, far]], axis=1
            )
            if t == 0:
                y_near = jnp.zeros((solved.shape[1], 2 * LANES), jnp.float32)
                y_far = y_near
            else:
                y_near = jnp.concatenate([solved[k0, :, near], solved[k1, :, near]], axis=1)
                y_far = jnp.concatenate([solved[k0, :, far], solved[k1, :, far]], axis=1)
                y_near = y_near.astype(jnp.float32)
                y_far = y_far.astype(jnp.float32)
            for j in range(pairs):
                low = jnp.concatenate([mine[j : j + 1]] * 2, axis=1)
                here = g * pairs + j - b * block_pairs
                own = wide_pair == here
                use_extra = jnp.logical_and(wide_extra, m == low)
                use_low = jnp.logical_and(jnp.logical_and(own, wide_member == 0), m <= low)
                use_high = jnp.logical_or(own, use_extra)
                lower = jnp.dot(matrices[g, 2 * j], x_near, preferred_element_type=jnp.float32)
                upper = jnp.dot(matrices[g, 2 * j + 1], x_near, preferred_element_type=jnp.float32)
                upper_far = jnp.dot(
                    matrices[g, 2 * j + 1], x_far, preferred_element_type=jnp.float32
                )
                y_near = jnp.where(use_low, lower, jnp.where(use_high, upper, y_near))
                y_far = jnp.where(use_extra, upper_far, y_far)
            y_near = y_near.astype(jnp.bfloat16)
            y_far = y_far.astype(jnp.bfloat16)
            solved[k0, :, near] = y_near[:, :LANES]
            solved[k1, :, near] = y_near[:, LANES:]
            solved[k0, :, far] = y_far[:, :LANES]
            solved[k1, :, far] = y_far[:, LANES:]
            if t == Z - 1:

                @pl.when(i > 0)
                def _():
                    back_copy(k0).start()

                back_copy(k1).start()
            return carry

        lax.fori_loop(0, W // 2, two_sources, 0)

    for t in range(Z):
        if t == Z - 1:
            relay(t)
        solve(t)

    total[...] = jnp.zeros_like(total)
    through_row = lax.broadcasted_iota(jnp.int32, (tail, levels), 0)
    through_lane = lax.broadcasted_iota(jnp.int32, (tail, levels), 1)
    response = jnp.concatenate(
        [
            jnp.where(through_lane == through_row + LANES, -1.0, 0.0),
            thermal_response[...].astype(jnp.float32),
            mass_row[...].astype(jnp.float32).reshape(1, levels),
        ],
        axis=0,
    ).astype(jnp.bfloat16)

    def collect(k, block):
        if not keep:
            build(k, 0)
        total[...] += lax.dot_general(
            block, pick[place_of(k)], (((1,), (1,)), ((), ())), preferred_element_type=jnp.float32
        )

    collect(0, solved[0])

    def gather_back(k, carry):
        back_copy(k).wait_recv()
        collect(k, returned[k])
        return carry

    lax.fori_loop(1, W, gather_back, 0)

    div = total[0:levels, :].astype(jnp.bfloat16)
    change = jnp.dot(response, div, preferred_element_type=jnp.float32)
    old = state[LANES:, :].astype(jnp.float32)
    below = lax.broadcasted_iota(jnp.int32, old.shape, 0) < tail
    new = jnp.where(below, 0.0, old) - change
    new = jnp.where(column_order >= 0, new, 0.0)
    out[0:LANES, :] = div[0:LANES, :]
    out[LANES:, :] = new.astype(jnp.bfloat16)

    def drain(k, carry):
        out_copy(k).wait_send()
        back_copy(k).wait_send()
        return carry

    lax.fori_loop(1, W, drain, 0)

    def drain_info(k, carry):
        info_copy(k).wait_send()
        return carry

    lax.fori_loop(1, devices, drain_info, 0)
    for g in range(Z):
        for c in range(chunks):

            @pl.when(jnp.logical_and(g <= z, z < Z - 1))
            def _():
                z_copy(g, c, 0).wait_send()

            @pl.when(jnp.logical_and(g >= z, z > 0))
            def _():
                z_copy(g, c, 1).wait_send()


def shards(
    state,
    held_orders,
    pair_lows,
    inverses,
    height_operator,
    pressure_column,
    thermal_response_matrix,
    mass_row,
):
    levels = height_operator.shape[0]
    slots = held_orders.shape[0]
    pairs = pair_lows.shape[0]
    Z, W = lax.axis_size("grp"), lax.axis_size("wave")
    devices = Z * W
    width = state.shape[1]
    rows = ceil_to(levels, ROWS_TILE)
    places = W if W * width * 4 * LANES <= KEEP_BYTES else 1
    vmem = pl.BlockSpec(memory_space=pltpu.VMEM)
    smem = pl.BlockSpec(memory_space=pltpu.SMEM)
    block = pltpu.VMEM((W, rows, 2 * LANES), jnp.bfloat16)
    return pl.pallas_call(
        functools.partial(kernel, (Z, W, levels, slots, pairs)),
        out_shape=jax.ShapeDtypeStruct(state.shape, jnp.bfloat16),
        in_specs=[smem, smem, pl.BlockSpec(memory_space=pl.ANY)] + [vmem] * 5,
        out_specs=vmem,
        scratch_shapes=[
            pltpu.VMEM(state.shape, jnp.bfloat16),
            pltpu.VMEM((devices, pairs + 1, LANES), jnp.int32),
            pltpu.VMEM((Z, 2 * pairs, rows, levels), jnp.bfloat16),
            pltpu.VMEM((Z, rows, LANES), jnp.bfloat16),
            pltpu.VMEM((rows, width), jnp.bfloat16),
            pltpu.VMEM((places, width, 2 * LANES), jnp.bfloat16),
            block,
            block,
            block,
            block,
            pltpu.VMEM((rows, width), jnp.float32),
            pltpu.SemaphoreType.DMA((devices,)),
            pltpu.SemaphoreType.DMA((devices,)),
            pltpu.SemaphoreType.DMA((Z, pairs + 1, 2)),
            pltpu.SemaphoreType.DMA((Z, pairs + 1)),
            pltpu.SemaphoreType.DMA((W,)),
            pltpu.SemaphoreType.DMA((W,)),
            pltpu.SemaphoreType.DMA((W,)),
            pltpu.SemaphoreType.DMA((W,)),
            pltpu.SemaphoreType.DMA,
        ],
        compiler_params=pltpu.CompilerParams(
            collective_id=0, has_side_effects=True, vmem_limit_bytes=60 * 1024 * 1024
        ),
    )(
        held_orders,
        pair_lows,
        state,
        inverses.reshape(2 * pairs, levels, levels),
        height_operator,
        pressure_column,
        thermal_response_matrix,
        mass_row,
    )


def solution(mesh):
    placed = (
        P(None, ("grp", "wave")),
        P(("grp", "wave")),
        P(("grp", "wave")),
        P(("grp", "wave"), None, None, None),
        P(),
        P(),
        P(),
        P(),
    )
    return jax.shard_map(
        shards, mesh=mesh, in_specs=placed, out_specs=P(None, ("grp", "wave")), check_vma=False
    )
```

profile of v0, /device:TPU:0, one launch (start us, length us, event | category | flops | bytes accessed | tf_op | source)
XLA Modules:
  0.0 50.6 jit_solution(1728221170699699864)
XLA Ops:
  0.0 1.8 %copy.9 = bf16[3,2,137,137]{3,2,1,0:T(8,128)(2,1)} copy(bf16[3,2,137,137]{3,1,2,0:T(2,128)(2,1)} %param.11) | data formatting | bytes 450456 | tf_op args[3]
  1.8 46.4 %shard_map.82 = bf16[275,1930]{1,0:T(8,128)(2,1)} custom-call(s32[5]{0:T(128)} %held.1, s32[3]{0:T(128)} %lows.1, bf16[275,1930]{1,0:T(8,128)(2,1)} %state_far.1, bf16[6,137,137]{2,1,0:T(8,128)(2,1)} %bitcast.1, bf16[137,137]{1,0:T(8,128)(2,1)} %height_operator.1, bf16[137]{0:T(256)(128)(2,1)} %pressure_column.1, bf16[137,137]{1,0:T(8,128)(2,1)} %thermal_response.1, ...), custom_call_target="tpu_custom_call" | custom-call | tf_op jit(solution)/shard_map/pallas_call | solution.py:434
  48.2 2.4 %copy.11 = bf16[275,1930]{1,0:T(8,128)(2,1)} copy(bf16[275,1930]{1,0:T(8,128)(2,1)} %shard_map.82) | data formatting | bytes 2123000
where the time goes:
time: 50.8 us; the launch traced here: 50.6 us
  Pallas kernels  46.4 us (91%)
  local copies, waits for them, and re-layouts  4.21 us (8%)
    pallas_call x1, Pallas kernels, shards(): pl.pallas_call(functools.partial(kernel, (Z, W, levels, slots, pairs)), o...  46.4 us
    unnamed x2, local copies, waits for them, and re-layouts  4.21 us

commit v1 on v0

v1 whole, which is shorter than its diff:
```python
import functools

import jax
import jax.numpy as jnp
from jax import lax
from jax.experimental import pallas as pl
from jax.experimental.pallas import tpu as pltpu
from jax.sharding import PartitionSpec as P

MESH = pl.DeviceIdType.MESH
LANES = 128
ROWS_TILE = 16
TABLE_ROWS = 8
KEEP_BYTES = 24 << 20
scope = jax.named_scope


def ceil_to(value, step):
    return -(-value // step) * step


def kernel(
    size,
    held,
    lows,
    state_far,
    inverses,
    height_operator,
    pressure_column,
    thermal_response,
    mass_row,
    out,
    state,
    info,
    low_table,
    matrices,
    rest,
    right,
    pick,
    outgoing,
    arrived,
    solved,
    returned,
    total,
    info_send,
    info_recv,
    table_send,
    table_recv,
    z_send,
    z_recv,
    out_send,
    out_recv,
    back_send,
    back_recv,
    state_sem,
):
    Z, W, levels, slots, pairs = size
    half_count = Z * W * pairs
    truncation = 2 * half_count - 1
    slot_width = 2 * (truncation + 2)
    width = slots * slot_width
    denom = float(truncation * (truncation + 1))
    per_pair = 4 * slots
    block_pairs = 2 * pairs
    first_extra = block_pairs * per_pair
    moved = per_pair - 2
    last_slot = slots - 1
    stages = W.bit_length() - 1
    tail = levels - LANES
    keep = pick.shape[1] > 1
    z = lax.axis_index("grp")
    w = lax.axis_index("wave")
    middle = jnp.logical_and(z > 0, z < Z - 1)

    def wave_peer(i):
        return w + (1 << i) * (1 - 2 * lax.rem(w // (1 << i), 2))

    barrier = pltpu.get_barrier_semaphore()
    for i in range(stages):
        pl.semaphore_signal(barrier, inc=1, device_id=(z, wave_peer(i)), device_id_type=MESH)
    for i in range(1, Z):
        pl.semaphore_signal(barrier, inc=1, device_id=(lax.rem(z + i, Z), w), device_id_type=MESH)
    fetch = pltpu.make_async_copy(state_far, state, state_sem)
    fetch.start()

    lane = lax.broadcasted_iota(jnp.int32, (1, LANES), 1)
    lane_pair = lane // per_pair
    lane_member = lax.rem(lane, per_pair) // (2 * slots)
    lane_slot = lax.rem(lax.rem(lane, per_pair), 2 * slots) // 2
    lane_part = lax.rem(lane, 2)
    spare = lane >= first_extra
    is_moved = jnp.logical_and(lane >= moved, lane < moved + 2)
    orders = jnp.full((1, LANES), -1, jnp.int32)
    for s in range(slots):
        orders = jnp.where(lane_slot == s, held[s], orders)
    low_row = jnp.zeros((1, LANES), jnp.int32)
    for j in range(pairs):
        low_row = jnp.where(lax.rem(lane_pair, pairs) == j, lows[j], low_row)
    table_row = lax.broadcasted_iota(jnp.int32, (TABLE_ROWS, LANES), 0)
    info[w] = jnp.where(table_row == 0, low_row, orders)

    ends = []
    for i in range(2 * pairs):
        matrices[z, i, 0:levels, :] = inverses[i]
        ends.append(inverses[i, :, LANES:levels].astype(jnp.float32))
    ends = jnp.concatenate(ends, axis=1).astype(jnp.bfloat16)
    rest[z, 0:levels, 0 : 2 * pairs * tail] = ends

    with scope("barrier"):
        pl.semaphore_wait(barrier, stages + Z - 1)

    def z_copy(g, c, way):
        if c < pairs:
            ref = matrices.at[g, pl.ds(2 * c, 2), :, pl.ds(0, LANES)]
        else:
            ref = rest.at[g]
        step = 1 if way == 0 else -1
        return pltpu.make_async_remote_copy(
            src_ref=ref,
            dst_ref=ref,
            send_sem=z_send.at[g, c, way],
            recv_sem=z_recv.at[g, c],
            device_id=(z + step, w),
            device_id_type=MESH,
        )

    def forward(g, c):
        @pl.when(jnp.logical_and(g <= z, z < Z - 1))
        def _():
            z_copy(g, c, 0).start()

        @pl.when(jnp.logical_and(g >= z, z > 0))
        def _():
            z_copy(g, c, 1).start()

    def group_at(t):
        g = z
        for zz in range(Z):
            by_distance = sorted(range(Z), key=lambda a: abs(a - zz))
            g = jnp.where(z == zz, by_distance[t], g)
        return g

    def relay(*steps):
        @pl.when(middle)
        def _():
            for t, c in steps:
                g = group_at(t)
                z_copy(g, c, 0).wait_recv()
                forward(g, c)

    def arrive(*steps):
        @pl.when(jnp.logical_not(middle))
        def _():
            for t, c in steps:
                z_copy(group_at(t), c, 0).wait_recv()

    def info_copy(i, start):
        ref = info.at[pl.ds(start, 1 << i)]
        return pltpu.make_async_remote_copy(
            src_ref=ref,
            dst_ref=ref,
            send_sem=info_send.at[i],
            recv_sem=info_recv.at[i],
            device_id=(z, wave_peer(i)),
            device_id_type=MESH,
        )

    def block_start(who, i):
        return who // (1 << i) * (1 << i)

    def table_copy(k):
        return pltpu.make_async_remote_copy(
            src_ref=low_table.at[z],
            dst_ref=low_table.at[z],
            send_sem=table_send.at[k],
            recv_sem=table_recv.at[k],
            device_id=(lax.rem(z + k, Z), w),
            device_id_type=MESH,
        )

    def table_arrival(k):
        ref = low_table.at[lax.rem(z + Z - k, Z)]
        return pltpu.make_async_remote_copy(
            src_ref=ref,
            dst_ref=ref,
            send_sem=table_send.at[k],
            recv_sem=table_recv.at[k],
            device_id=(lax.rem(z + Z - k, Z), w),
            device_id_type=MESH,
        )

    forward(z, pairs)
    forward(z, 0)
    with scope("info0"):
        info_copy(0, block_start(w, 0)).start()

    column = lax.broadcasted_iota(jnp.int32, (1, width), 1)
    column_order = jnp.full((1, width), -1, jnp.int32)
    column_start = jnp.zeros((1, width), jnp.int32)
    for s in range(slots):
        inside = jnp.logical_and(column >= s * slot_width, column < (s + 1) * slot_width)
        column_order = jnp.where(inside, held[s], column_order)
        column_start = jnp.where(inside, s * slot_width, column_start)

    def drive_right():
        coefficient = (column - column_start) // 2
        degree = jnp.where(
            coefficient <= truncation - column_order, column_order + coefficient, coefficient - 1
        )
        lap_scale = (degree * (degree + 1)).astype(jnp.float32) / denom
        height = height_operator[...].astype(jnp.float32)
        pressure_row = jnp.broadcast_to(
            pressure_column[...].astype(jnp.float32).reshape(1, levels), height.shape
        )
        across = lax.broadcasted_iota(jnp.int32, height.shape, 1)
        down = lax.broadcasted_iota(jnp.int32, height.shape, 0)
        pressure_side = jnp.sum(
            jnp.where(across == down, pressure_row, 0.0), axis=1, keepdims=True
        )
        height = jnp.concatenate(
            [jnp.zeros((levels, tail), jnp.float32), height, pressure_side], axis=1
        ).astype(jnp.bfloat16)
        fetch.wait()
        drive = jnp.dot(height, state[LANES:, :], preferred_element_type=jnp.float32)
        right[0:levels, :] = (
            state[0:levels, :].astype(jnp.float32) + lap_scale * drive
        ).astype(jnp.bfloat16)

    for i in range(stages):
        with scope(f"info_wait{i}"):
            info_copy(i, block_start(wave_peer(i), i)).wait_recv()
        if i + 1 < stages:
            info_copy(i + 1, block_start(w, i + 1)).start()
        if i == 0:
            with scope("drive"):
                drive_right()
        if i == 1:
            for c in range(1, pairs - 1):
                forward(z, c)

    for d in range(W):
        low_table[z, d : d + 1, :] = info[d, 0:1, :]
    for k in range(1, Z):
        table_copy(k).start()
    for c in range(pairs - 1, pairs):
        forward(z, c)
    with scope("relay_a"):
        relay((1, pairs), (2, pairs), (1, 0), (2, 0))
    with scope("table_wait"):
        for k in range(1, Z):
            table_arrival(k).wait_recv()

    groups = [group_at(t) for t in range(Z)]

    def target_of(b, k):
        d = lax.rem(w + k, W)
        rows = [low_table[groups[t], pl.ds(d, 1), :] for t in range(Z)]
        low = jnp.where(lane < pairs * per_pair, rows[2 * b], rows[2 * b + 1])
        slot, member, order = lane_slot, lane_member, orders
        if b == 0:
            low = jnp.where(spare, rows[2], low)
            slot = jnp.where(spare, last_slot, slot)
            member = jnp.where(spare, 1, member)
            order = jnp.where(spare, held[last_slot], order)
        merged = jnp.where(order <= low, low - order, truncation + 1 - low)
        position = jnp.where(member == 0, merged, truncation - low - order)
        used = order >= 0
        if b == 0:
            used = jnp.logical_and(used, lane < first_extra + 2)
        else:
            extra = jnp.logical_or(spare, is_moved)
            position = jnp.where(extra, truncation + 1 - order, position)
        target = slot * slot_width + 2 * position + lane_part
        return jnp.where(used, target, -1)

    def build(b, i, place):
        at = lax.broadcasted_iota(jnp.int32, (width, LANES), 0)
        for h in range(2):
            pick[b, place, :, h * LANES : (h + 1) * LANES] = jnp.where(
                at == target_of(b, 2 * i + h), 1.0, 0.0
            ).astype(jnp.bfloat16)

    def place_of(i):
        return i if keep else 0

    def out_copy(b, k):
        return pltpu.make_async_remote_copy(
            src_ref=outgoing.at[b, k],
            dst_ref=arrived.at[b, k],
            send_sem=out_send.at[b, k],
            recv_sem=out_recv.at[b, k],
            device_id=(z, lax.rem(w + k, W)),
            device_id_type=MESH,
        )

    def back_copy(b, k):
        return pltpu.make_async_remote_copy(
            src_ref=solved.at[b, k],
            dst_ref=returned.at[b, k],
            send_sem=back_send.at[b, k],
            recv_sem=back_recv.at[b, k],
            device_id=(z, lax.rem(w + W - k, W)),
            device_id_type=MESH,
        )

    def send_block(b):
        def send(i, carry):
            build(b, i, place_of(i))
            message = jnp.dot(
                right[...], pick[b, place_of(i)], preferred_element_type=jnp.float32
            ).astype(jnp.bfloat16)
            k0, k1 = 2 * i, 2 * i + 1
            outgoing[b, k0] = message[:, :LANES]
            outgoing[b, k1] = message[:, LANES:]

            @pl.when(i > 0)
            def _():
                out_copy(b, k0).start()

            out_copy(b, k1).start()
            return carry

        lax.fori_loop(0, W // 2, send, 0)
        arrived[b, 0] = outgoing[b, 0]

    def wait_block(b):
        def wait_out(k, carry):
            out_copy(b, k).wait_recv()
            return carry

        lax.fori_loop(1, W, wait_out, 0)

    with scope("send0"):
        send_block(0)
    with scope("relay_b"):
        for c in range(1, pairs):
            relay((1, c), (2, c))
    with scope("send1"):
        send_block(1)
    with scope("relay_c"):
        relay((3, pairs), (3, 0))

    def low_values():
        rows = []
        for t in range(Z):
            row = low_table[groups[t], pl.ds(w, 1), :]
            for j in range(pairs):
                rows.append(jnp.where(lane_pair == j, row, -1).astype(jnp.float32))
        return jnp.max(jnp.concatenate(rows, axis=0), axis=1, keepdims=True).astype(jnp.int32)

    low_column = low_values()

    def low_at(t, j):
        return low_column[t * pairs + j : t * pairs + j + 1, :]

    def twice(row):
        return jnp.concatenate([row, row], axis=1)

    wide_pair = twice(lane_pair)
    wide_member = twice(lane_member)
    wide_spare = twice(spare)
    wide_extra = twice(jnp.logical_or(spare, is_moved))

    def fill_rest(t):
        g = groups[t]
        for i in range(2 * pairs):
            piece = rest[g].astype(jnp.float32)[:, i * tail : (i + 1) * tail]
            matrices[g, i, :, LANES:levels] = piece.astype(jnp.bfloat16)

    def columns(buffer, b, i, count):
        return jnp.concatenate(
            [buffer[b, 2 * i, 0:count, :], buffer[b, 2 * i + 1, 0:count, :]], axis=1
        )

    def store(b, i, y):
        y = y.astype(jnp.bfloat16)
        solved[b, 2 * i] = y[:, :LANES]
        solved[b, 2 * i + 1] = y[:, LANES:]

    def source_orders(i):
        s0 = lax.rem(w + W - 2 * i, W)
        s1 = lax.rem(w + W - 2 * i - 1, W)
        return jnp.concatenate([info[s0][1:2], info[s1][1:2]], axis=1)

    def times(t, j, member, x):
        return jnp.dot(
            matrices[groups[t], 2 * j + member], x, preferred_element_type=jnp.float32
        )

    rows = solved.shape[2]

    def regular(b, t, j, m, x, y):
        own = wide_pair == (t - 2 * b) * pairs + j
        low = low_at(t, j)
        if b == 1:
            extra = jnp.logical_and(wide_extra, m == low)
            own = jnp.logical_and(own, jnp.logical_not(wide_extra))
        use_low = jnp.logical_and(jnp.logical_and(own, wide_member == 0), m <= low)
        use_high = jnp.logical_or(own, extra) if b == 1 else own
        lower = times(t, j, 0, x)
        upper = times(t, j, 1, x)
        return jnp.where(use_low, lower, jnp.where(use_high, upper, y))

    def near(i, carry):
        m = source_orders(i)
        x = columns(arrived, 0, i, levels)
        y = jnp.zeros((rows, 2 * LANES), jnp.float32)
        for t in range(2):
            for j in range(pairs):
                y = regular(0, t, j, m, x, y)
        store(0, i, y)
        return carry

    def send_back(b, i):
        @pl.when(i > 0)
        def _():
            back_copy(b, 2 * i).start()

        back_copy(b, 2 * i + 1).start()

    def turn(i, carry):
        m = source_orders(i)
        x = columns(arrived, 1, i, levels)
        y = jnp.zeros((rows, 2 * LANES), jnp.float32)
        for t in range(2):
            for j in range(pairs):
                extra = jnp.logical_and(wide_extra, m == low_at(t, j))
                y = jnp.where(extra, times(t, j, 1, x), y)
        y = regular(1, 2, 0, m, x, y)
        store(1, i, y)
        y = columns(solved, 0, i, rows).astype(jnp.float32)
        y = jnp.where(wide_spare, times(2, 0, 1, columns(arrived, 0, i, levels)), y)
        store(0, i, y)
        send_back(0, i)
        return carry

    def late(steps, last):
        def body(i, carry):
            m = source_orders(i)
            x = columns(arrived, 1, i, levels)
            y = columns(solved, 1, i, rows).astype(jnp.float32)
            for t, j in steps:
                y = regular(1, t, j, m, x, y)
            store(1, i, y)
            if last:
                send_back(1, i)
            return carry

        lax.fori_loop(0, W // 2, body, 0)

    with scope("wait0"):
        wait_block(0)
        arrive((1, pairs), *[(1, c) for c in range(pairs)])
    fill_rest(1)
    with scope("near"):
        lax.fori_loop(0, W // 2, near, 0)
    with scope("relay_d"):
        relay(*[(3, c) for c in range(1, pairs)])
    with scope("wait1"):
        wait_block(1)
    with scope("arrive2"):
        arrive((2, pairs), (2, 0))
    fill_rest(2)
    with scope("turn"):
        lax.fori_loop(0, W // 2, turn, 0)
    with scope("arrive2b"):
        arrive(*[(2, c) for c in range(1, pairs)])
    with scope("late2"):
        late([(2, j) for j in range(1, pairs)], False)
    with scope("arrive3"):
        arrive((3, pairs), *[(3, c) for c in range(pairs - 1)])
    fill_rest(3)
    with scope("late3"):
        late([(3, j) for j in range(pairs - 1)], False)
    with scope("arrive3b"):
        arrive((3, pairs - 1))
    with scope("late3b"):
        late([(3, pairs - 1)], True)

    total[...] = jnp.zeros_like(total)
    through_row = lax.broadcasted_iota(jnp.int32, (tail, levels), 0)
    through_lane = lax.broadcasted_iota(jnp.int32, (tail, levels), 1)
    response = jnp.concatenate(
        [
            jnp.where(through_lane == through_row + LANES, -1.0, 0.0),
            thermal_response[...].astype(jnp.float32),
            mass_row[...].astype(jnp.float32).reshape(1, levels),
        ],
        axis=0,
    ).astype(jnp.bfloat16)

    def collect(b, i, first, second):
        if not keep:
            build(b, i, 0)
        total[...] += lax.dot_general(
            jnp.concatenate([first, second], axis=1),
            pick[b, place_of(i)],
            (((1,), (1,)), ((), ())),
            preferred_element_type=jnp.float32,
        )

    def gather_back(b):
        with scope(f"back{b}_0"):
            back_copy(b, 1).wait_recv()
            collect(b, 0, solved[b, 0], returned[b, 1])

        def step(i, carry):
            back_copy(b, 2 * i).wait_recv()
            back_copy(b, 2 * i + 1).wait_recv()
            collect(b, i, returned[b, 2 * i], returned[b, 2 * i + 1])
            return carry

        with scope(f"back{b}"):
            lax.fori_loop(1, W // 2, step, 0)

    gather_back(0)
    gather_back(1)

    with scope("final"):
        div = total[0:levels, :].astype(jnp.bfloat16)
        change = jnp.dot(response, div, preferred_element_type=jnp.float32)
        old = state[LANES:, :].astype(jnp.float32)
        below = lax.broadcasted_iota(jnp.int32, old.shape, 0) < tail
        new = jnp.where(below, 0.0, old) - change
        new = jnp.where(column_order >= 0, new, 0.0)
        out[0:LANES, :] = div[0:LANES, :]
        out[LANES:, :] = new.astype(jnp.bfloat16)

    def drain(k, carry):
        for b in range(2):
            out_copy(b, k).wait_send()
            back_copy(b, k).wait_send()
        return carry

    lax.fori_loop(1, W, drain, 0)
    for i in range(stages):
        info_copy(i, block_start(w, i)).wait_send()
    for k in range(1, Z):
        table_copy(k).wait_send()
    for g in range(Z):
        for c in range(pairs + 1):

            @pl.when(jnp.logical_and(g <= z, z < Z - 1))
            def _():
                z_copy(g, c, 0).wait_send()

            @pl.when(jnp.logical_and(g >= z, z > 0))
            def _():
                z_copy(g, c, 1).wait_send()


def shards(
    state,
    held_orders,
    pair_lows,
    inverses,
    height_operator,
    pressure_column,
    thermal_response_matrix,
    mass_row,
):
    levels = height_operator.shape[0]
    slots = held_orders.shape[0]
    pairs = pair_lows.shape[0]
    Z, W = lax.axis_size("grp"), lax.axis_size("wave")
    width = state.shape[1]
    rows = ceil_to(levels, ROWS_TILE)
    places = W // 2 if W * width * 4 * LANES <= KEEP_BYTES else 1
    stages = W.bit_length() - 1
    vmem = pl.BlockSpec(memory_space=pltpu.VMEM)
    smem = pl.BlockSpec(memory_space=pltpu.SMEM)
    block = pltpu.VMEM((2, W, rows, LANES), jnp.bfloat16)
    return pl.pallas_call(
        functools.partial(kernel, (Z, W, levels, slots, pairs)),
        out_shape=jax.ShapeDtypeStruct(state.shape, jnp.bfloat16),
        in_specs=[smem, smem, pl.BlockSpec(memory_space=pl.ANY)] + [vmem] * 5,
        out_specs=vmem,
        scratch_shapes=[
            pltpu.VMEM(state.shape, jnp.bfloat16),
            pltpu.VMEM((W, TABLE_ROWS, LANES), jnp.int32),
            pltpu.VMEM((Z, W, LANES), jnp.int32),
            pltpu.VMEM((Z, 2 * pairs, rows, levels), jnp.bfloat16),
            pltpu.VMEM((Z, rows, LANES), jnp.bfloat16),
            pltpu.VMEM((rows, width), jnp.bfloat16),
            pltpu.VMEM((2, places, width, 2 * LANES), jnp.bfloat16),
            block,
            block,
            block,
            block,
            pltpu.VMEM((rows, width), jnp.float32),
            pltpu.SemaphoreType.DMA((stages,)),
            pltpu.SemaphoreType.DMA((stages,)),
            pltpu.SemaphoreType.DMA((Z,)),
            pltpu.SemaphoreType.DMA((Z,)),
            pltpu.SemaphoreType.DMA((Z, pairs + 1, 2)),
            pltpu.SemaphoreType.DMA((Z, pairs + 1)),
            pltpu.SemaphoreType.DMA((2, W)),
            pltpu.SemaphoreType.DMA((2, W)),
            pltpu.SemaphoreType.DMA((2, W)),
            pltpu.SemaphoreType.DMA((2, W)),
            pltpu.SemaphoreType.DMA,
        ],
        compiler_params=pltpu.CompilerParams(
            collective_id=0, has_side_effects=True, vmem_limit_bytes=60 * 1024 * 1024
        ),
    )(
        held_orders,
        pair_lows,
        state,
        inverses.reshape(2 * pairs, levels, levels),
        height_operator,
        pressure_column,
        thermal_response_matrix,
        mass_row,
    )


def solution(mesh):
    placed = (
        P(None, ("grp", "wave")),
        P(("grp", "wave")),
        P(("grp", "wave")),
        P(("grp", "wave"), None, None, None),
        P(),
        P(),
        P(),
        P(),
    )
    return jax.shard_map(
        shards, mesh=mesh, in_specs=placed, out_specs=P(None, ("grp", "wave")), check_vma=False
    )
```

time: 50.8 us -> 42.2 us (0.83)
  Pallas kernels: 46.4 us -> 37.7 us
    pallas_call x1, Pallas kernels: 46.4 us -> 37.7 us  [shards(): pl.pallas_call(functools.partial(kernel, (Z, W, levels, slots, pairs)), o...]
where the time goes in v1:
time: 42.2 us; the launch traced here: 42 us
  Pallas kernels  37.7 us (89%)
  local copies, waits for them, and re-layouts  4.21 us (10%)
    pallas_call x1, Pallas kernels, shards(): pl.pallas_call(functools.partial(kernel, (Z, W, levels, slots, pairs)), o...  37.7 us
    unnamed x2, local copies, waits for them, and re-layouts  4.21 us

profile of v1, /device:TPU:0, one launch (start us, length us, event | category | flops | bytes accessed | tf_op | source)
XLA Modules:
  0.0 42.0 jit_solution(7668876049879948727)
XLA Ops:
  0.0 1.8 %copy.9 = bf16[3,2,137,137]{3,2,1,0:T(8,128)(2,1)} copy(bf16[3,2,137,137]{3,1,2,0:T(2,128)(2,1)} %param.11) | data formatting | bytes 450456 | tf_op args[3]
  1.8 37.7 %shard_map.82 = bf16[275,1930]{1,0:T(8,128)(2,1)} custom-call(s32[5]{0:T(128)} %held.1, s32[3]{0:T(128)} %lows.1, bf16[275,1930]{1,0:T(8,128)(2,1)} %state_far.1, bf16[6,137,137]{2,1,0:T(8,128)(2,1)} %bitcast.1, bf16[137,137]{1,0:T(8,128)(2,1)} %height_operator.1, bf16[137]{0:T(256)(128)(2,1)} %pressure_column.1, bf16[137,137]{1,0:T(8,128)(2,1)} %thermal_response.1, ...), custom_call_target="tpu_custom_call" | custom-call | tf_op jit(solution)/shard_map/pallas_call | solution.py:573
  39.6 2.4 %copy.11 = bf16[275,1930]{1,0:T(8,128)(2,1)} copy(bf16[275,1930]{1,0:T(8,128)(2,1)} %shard_map.82) | data formatting | bytes 2123000

commit v2 on v1

--- a/solution.py
+++ b/solution.py
@@ -21,18 +21,25 @@
 
 def kernel(
     size,
+    held_far,
+    lows_far,
+    state_far,
+    inverses_far,
+    height_far,
+    pressure_far,
+    thermal_far,
+    mass_far,
+    out,
     held,
     lows,
-    state_far,
+    state,
     inverses,
     height_operator,
     pressure_column,
     thermal_response,
     mass_row,
-    out,
-    state,
+    low_rows,
     info,
-    low_table,
     matrices,
     rest,
     right,
@@ -42,17 +49,17 @@
     solved,
     returned,
     total,
+    row_send,
+    row_recv,
     info_send,
     info_recv,
-    table_send,
-    table_recv,
     z_send,
     z_recv,
     out_send,
     out_recv,
     back_send,
     back_recv,
-    state_sem,
+    fetch_sem,
 ):
     Z, W, levels, slots, pairs = size
     half_count = Z * W * pairs
@@ -65,23 +72,42 @@
     first_extra = block_pairs * per_pair
     moved = per_pair - 2
     last_slot = slots - 1
-    stages = W.bit_length() - 1
     tail = levels - LANES
     keep = pick.shape[1] > 1
     z = lax.axis_index("grp")
     w = lax.axis_index("wave")
     middle = jnp.logical_and(z > 0, z < Z - 1)
 
-    def wave_peer(i):
-        return w + (1 << i) * (1 - 2 * lax.rem(w // (1 << i), 2))
-
     barrier = pltpu.get_barrier_semaphore()
-    for i in range(stages):
-        pl.semaphore_signal(barrier, inc=1, device_id=(z, wave_peer(i)), device_id_type=MESH)
-    for i in range(1, Z):
-        pl.semaphore_signal(barrier, inc=1, device_id=(lax.rem(z + i, Z), w), device_id_type=MESH)
-    fetch = pltpu.make_async_copy(state_far, state, state_sem)
-    fetch.start()
+
+    def greet(k, carry):
+        pl.semaphore_signal(
+            barrier, inc=1, device_id=(z, lax.rem(w + k, W)), device_id_type=MESH
+        )
+        return carry
+
+    fetches = [
+        pltpu.make_async_copy(far, near, fetch_sem.at[i])
+        for i, (far, near) in enumerate(
+            [
+                (lows_far, lows),
+                (held_far, held),
+                (inverses_far, inverses),
+                (state_far, state),
+                (height_far, height_operator),
+                (pressure_far, pressure_column),
+                (thermal_far, thermal_response),
+                (mass_far, mass_row),
+            ]
+        )
+    ]
+    for k in range(1, Z):
+        pl.semaphore_signal(barrier, inc=1, device_id=(lax.rem(z + k, Z), w), device_id_type=MESH)
+    for fetch in fetches[:3]:
+        fetch.start()
+    lax.fori_loop(1, W, greet, 0)
+    for fetch in fetches[3:]:
+        fetch.start()
 
     lane = lax.broadcasted_iota(jnp.int32, (1, LANES), 1)
     lane_pair = lane // per_pair
@@ -90,24 +116,40 @@
     lane_part = lax.rem(lane, 2)
     spare = lane >= first_extra
     is_moved = jnp.logical_and(lane >= moved, lane < moved + 2)
+    with scope("small_fetch"):
+        fetches[0].wait()
+        fetches[1].wait()
     orders = jnp.full((1, LANES), -1, jnp.int32)
     for s in range(slots):
         orders = jnp.where(lane_slot == s, held[s], orders)
     low_row = jnp.zeros((1, LANES), jnp.int32)
     for j in range(pairs):
         low_row = jnp.where(lax.rem(lane_pair, pairs) == j, lows[j], low_row)
-    table_row = lax.broadcasted_iota(jnp.int32, (TABLE_ROWS, LANES), 0)
-    info[w] = jnp.where(table_row == 0, low_row, orders)
-
-    ends = []
-    for i in range(2 * pairs):
-        matrices[z, i, 0:levels, :] = inverses[i]
-        ends.append(inverses[i, :, LANES:levels].astype(jnp.float32))
-    ends = jnp.concatenate(ends, axis=1).astype(jnp.bfloat16)
-    rest[z, 0:levels, 0 : 2 * pairs * tail] = ends
+    low_rows[z] = jnp.broadcast_to(low_row, (TABLE_ROWS, LANES))
+
+    with scope("inverse_fetch"):
+        fetches[2].wait()
+    rows = matrices.shape[2]
+    with scope("split"):
+        to_row = lax.broadcasted_iota(jnp.int32, (2 * rows, 2 * levels), 0)
+        from_row = lax.broadcasted_iota(jnp.int32, (2 * rows, 2 * levels), 1)
+        wanted = jnp.where(to_row < rows, 2 * to_row, 2 * (to_row - rows) + 1)
+        split = jnp.where(wanted == from_row, 1.0, 0.0).astype(jnp.bfloat16)
+        ends = []
+        for j in range(pairs):
+            both = jnp.dot(
+                split,
+                inverses[j].reshape(2 * levels, levels),
+                preferred_element_type=jnp.float32,
+            )
+            for member in range(2):
+                matrix = both[member * rows : (member + 1) * rows]
+                matrices[z, 2 * j + member] = matrix.astype(jnp.bfloat16)
+                ends.append(matrix[:, LANES:levels])
+        rest[z, :, 0 : 2 * pairs * tail] = jnp.concatenate(ends, axis=1).astype(jnp.bfloat16)
 
     with scope("barrier"):
-        pl.semaphore_wait(barrier, stages + Z - 1)
+        pl.semaphore_wait(barrier, W + Z - 2)
 
     def z_copy(g, c, way):
         if c < pairs:
@@ -154,45 +196,52 @@
             for t, c in steps:
                 z_copy(group_at(t), c, 0).wait_recv()
 
-    def info_copy(i, start):
-        ref = info.at[pl.ds(start, 1 << i)]
+    def row_copy(k):
         return pltpu.make_async_remote_copy(
-            src_ref=ref,
-            dst_ref=ref,
-            send_sem=info_send.at[i],
-            recv_sem=info_recv.at[i],
-            device_id=(z, wave_peer(i)),
-            device_id_type=MESH,
-        )
-
-    def block_start(who, i):
-        return who // (1 << i) * (1 << i)
-
-    def table_copy(k):
-        return pltpu.make_async_remote_copy(
-            src_ref=low_table.at[z],
-            dst_ref=low_table.at[z],
-            send_sem=table_send.at[k],
-            recv_sem=table_recv.at[k],
+            src_ref=low_rows.at[z],
+            dst_ref=low_rows.at[z],
+            send_sem=row_send.at[k],
+            recv_sem=row_recv.at[k],
             device_id=(lax.rem(z + k, Z), w),
             device_id_type=MESH,
         )
 
-    def table_arrival(k):
-        ref = low_table.at[lax.rem(z + Z - k, Z)]
+    def row_arrival(k):
+        source = lax.rem(z + Z - k, Z)
         return pltpu.make_async_remote_copy(
-            src_ref=ref,
-            dst_ref=ref,
-            send_sem=table_send.at[k],
-            recv_sem=table_recv.at[k],
-            device_id=(lax.rem(z + Z - k, Z), w),
+            src_ref=low_rows.at[source],
+            dst_ref=low_rows.at[source],
+            send_sem=row_send.at[k],
+            recv_sem=row_recv.at[k],
+            device_id=(source, w),
             device_id_type=MESH,
         )
 
-    forward(z, pairs)
-    forward(z, 0)
-    with scope("info0"):
-        info_copy(0, block_start(w, 0)).start()
+    def info_copy(k):
+        return pltpu.make_async_remote_copy(
+            src_ref=info.at[w],
+            dst_ref=info.at[w],
+            send_sem=info_send.at[k],
+            recv_sem=info_recv.at[k],
+            device_id=(z, lax.rem(w + k, W)),
+            device_id_type=MESH,
+        )
+
+    def info_arrival(k):
+        source = lax.rem(w + W - k, W)
+        return pltpu.make_async_remote_copy(
+            src_ref=info.at[source],
+            dst_ref=info.at[source],
+            send_sem=info_send.at[k],
+            recv_sem=info_recv.at[k],
+            device_id=(z, source),
+            device_id_type=MESH,
+        )
+
+    for k in range(1, Z):
+        row_copy(k).start()
+    for c in [pairs, *range(pairs)]:
+        forward(z, c)
 
     column = lax.broadcasted_iota(jnp.int32, (1, width), 1)
     column_order = jnp.full((1, width), -1, jnp.int32)
@@ -208,6 +257,8 @@
             coefficient <= truncation - column_order, column_order + coefficient, coefficient - 1
         )
         lap_scale = (degree * (degree + 1)).astype(jnp.float32) / denom
+        fetches[4].wait()
+        fetches[5].wait()
         height = height_operator[...].astype(jnp.float32)
         pressure_row = jnp.broadcast_to(
             pressure_column[...].astype(jnp.float32).reshape(1, levels), height.shape
@@ -220,41 +271,39 @@
         height = jnp.concatenate(
             [jnp.zeros((levels, tail), jnp.float32), height, pressure_side], axis=1
         ).astype(jnp.bfloat16)
-        fetch.wait()
+        fetches[3].wait()
         drive = jnp.dot(height, state[LANES:, :], preferred_element_type=jnp.float32)
         right[0:levels, :] = (
             state[0:levels, :].astype(jnp.float32) + lap_scale * drive
         ).astype(jnp.bfloat16)
 
-    for i in range(stages):
-        with scope(f"info_wait{i}"):
-            info_copy(i, block_start(wave_peer(i), i)).wait_recv()
-        if i + 1 < stages:
-            info_copy(i + 1, block_start(w, i + 1)).start()
-        if i == 0:
-            with scope("drive"):
-                drive_right()
-        if i == 1:
-            for c in range(1, pairs - 1):
-                forward(z, c)
-
-    for d in range(W):
-        low_table[z, d : d + 1, :] = info[d, 0:1, :]
-    for k in range(1, Z):
-        table_copy(k).start()
-    for c in range(pairs - 1, pairs):
-        forward(z, c)
-    with scope("relay_a"):
-        relay((1, pairs), (2, pairs), (1, 0), (2, 0))
-    with scope("table_wait"):
+    with scope("rows_wait"):
         for k in range(1, Z):
-            table_arrival(k).wait_recv()
+            row_arrival(k).wait_recv()
+    table = [low_rows[g][0:1] for g in range(Z)]
+    table += [jnp.broadcast_to(orders, (TABLE_ROWS - Z, LANES))]
+    info[w] = jnp.concatenate(table, axis=0)
+
+    def start_info(k, carry):
+        info_copy(k).start()
+        return carry
+
+    lax.fori_loop(1, W, start_info, 0)
+    with scope("drive"):
+        drive_right()
+
+    def wait_info(k, carry):
+        info_arrival(k).wait_recv()
+        return carry
+
+    with scope("info_wait"):
+        lax.fori_loop(1, W, wait_info, 0)
 
     groups = [group_at(t) for t in range(Z)]
 
     def target_of(b, k):
         d = lax.rem(w + k, W)
-        rows = [low_table[groups[t], pl.ds(d, 1), :] for t in range(Z)]
+        rows = [info[d, pl.ds(groups[t], 1), :] for t in range(Z)]
         low = jnp.where(lane < pairs * per_pair, rows[2 * b], rows[2 * b + 1])
         slot, member, order = lane_slot, lane_member, orders
         if b == 0:
@@ -330,6 +379,8 @@
 
         lax.fori_loop(1, W, wait_out, 0)
 
+    with scope("relay_a"):
+        relay((1, pairs), (2, pairs), (1, 0), (2, 0))
     with scope("send0"):
         send_block(0)
     with scope("relay_b"):
@@ -343,7 +394,7 @@
     def low_values():
         rows = []
         for t in range(Z):
-            row = low_table[groups[t], pl.ds(w, 1), :]
+            row = info[w, pl.ds(groups[t], 1), :]
             for j in range(pairs):
                 rows.append(jnp.where(lane_pair == j, row, -1).astype(jnp.float32))
         return jnp.max(jnp.concatenate(rows, axis=0), axis=1, keepdims=True).astype(jnp.int32)
@@ -380,14 +431,12 @@
     def source_orders(i):
         s0 = lax.rem(w + W - 2 * i, W)
         s1 = lax.rem(w + W - 2 * i - 1, W)
-        return jnp.concatenate([info[s0][1:2], info[s1][1:2]], axis=1)
+        return jnp.concatenate([info[s0][Z : Z + 1], info[s1][Z : Z + 1]], axis=1)
 
     def times(t, j, member, x):
         return jnp.dot(
             matrices[groups[t], 2 * j + member], x, preferred_element_type=jnp.float32
         )
-
-    rows = solved.shape[2]
 
     def regular(b, t, j, m, x, y):
         own = wide_pair == (t - 2 * b) * pairs + j
@@ -477,6 +526,8 @@
     with scope("late3b"):
         late([(3, pairs - 1)], True)
 
+    fetches[6].wait()
+    fetches[7].wait()
     total[...] = jnp.zeros_like(total)
     through_row = lax.broadcasted_iota(jnp.int32, (tail, levels), 0)
     through_lane = lax.broadcasted_iota(jnp.int32, (tail, levels), 1)
@@ -533,10 +584,14 @@
         return carry
 
     lax.fori_loop(1, W, drain, 0)
-    for i in range(stages):
-        info_copy(i, block_start(w, i)).wait_send()
     for k in range(1, Z):
-        table_copy(k).wait_send()
+        row_copy(k).wait_send()
+
+    def drain_info(k, carry):
+        info_copy(k).wait_send()
+        return carry
+
+    lax.fori_loop(1, W, drain_info, 0)
     for g in range(Z):
         for c in range(pairs + 1):
 
@@ -566,19 +621,23 @@
     width = state.shape[1]
     rows = ceil_to(levels, ROWS_TILE)
     places = W // 2 if W * width * 4 * LANES <= KEEP_BYTES else 1
-    stages = W.bit_length() - 1
-    vmem = pl.BlockSpec(memory_space=pltpu.VMEM)
-    smem = pl.BlockSpec(memory_space=pltpu.SMEM)
     block = pltpu.VMEM((2, W, rows, LANES), jnp.bfloat16)
     return pl.pallas_call(
         functools.partial(kernel, (Z, W, levels, slots, pairs)),
         out_shape=jax.ShapeDtypeStruct(state.shape, jnp.bfloat16),
-        in_specs=[smem, smem, pl.BlockSpec(memory_space=pl.ANY)] + [vmem] * 5,
-        out_specs=vmem,
+        in_specs=[pl.BlockSpec(memory_space=pl.ANY)] * 8,
+        out_specs=pl.BlockSpec(memory_space=pltpu.VMEM),
         scratch_shapes=[
+            pltpu.SMEM(held_orders.shape, jnp.int32),
+            pltpu.SMEM(pair_lows.shape, jnp.int32),
             pltpu.VMEM(state.shape, jnp.bfloat16),
+            pltpu.VMEM((pairs, levels, 2, levels), jnp.bfloat16),
+            pltpu.VMEM(height_operator.shape, jnp.bfloat16),
+            pltpu.VMEM(pressure_column.shape, jnp.bfloat16),
+            pltpu.VMEM(thermal_response_matrix.shape, jnp.bfloat16),
+            pltpu.VMEM(mass_row.shape, jnp.bfloat16),
+            pltpu.VMEM((Z, TABLE_ROWS, LANES), jnp.int32),
             pltpu.VMEM((W, TABLE_ROWS, LANES), jnp.int32),
-            pltpu.VMEM((Z, W, LANES), jnp.int32),
             pltpu.VMEM((Z, 2 * pairs, rows, levels), jnp.bfloat16),
             pltpu.VMEM((Z, rows, LANES), jnp.bfloat16),
             pltpu.VMEM((rows, width), jnp.bfloat16),
@@ -588,17 +647,17 @@
             block,
             block,
             pltpu.VMEM((rows, width), jnp.float32),
-            pltpu.SemaphoreType.DMA((stages,)),
-            pltpu.SemaphoreType.DMA((stages,)),
             pltpu.SemaphoreType.DMA((Z,)),
             pltpu.SemaphoreType.DMA((Z,)),
+            pltpu.SemaphoreType.DMA((W,)),
+            pltpu.SemaphoreType.DMA((W,)),
             pltpu.SemaphoreType.DMA((Z, pairs + 1, 2)),
             pltpu.SemaphoreType.DMA((Z, pairs + 1)),
             pltpu.SemaphoreType.DMA((2, W)),
             pltpu.SemaphoreType.DMA((2, W)),
             pltpu.SemaphoreType.DMA((2, W)),
             pltpu.SemaphoreType.DMA((2, W)),
-            pltpu.SemaphoreType.DMA,
+            pltpu.SemaphoreType.DMA((8,)),
         ],
         compiler_params=pltpu.CompilerParams(
             collective_id=0, has_side_effects=True, vmem_limit_bytes=60 * 1024 * 1024
@@ -607,7 +666,7 @@
         held_orders,
         pair_lows,
         state,
-        inverses.reshape(2 * pairs, levels, levels),
+        jnp.transpose(inverses, (0, 2, 1, 3)),
         height_operator,
         pressure_column,
         thermal_response_matrix,

time: 42.2 us -> 37.6 us (0.89)
  Pallas kernels: 37.7 us -> 35.1 us
  local copies, waits for them, and re-layouts: 4.21 us -> 2.39 us
    pallas_call x1, Pallas kernels: 37.7 us -> 35.1 us  [shards(): pl.pallas_call(functools.partial(kernel, (Z, W, levels, slots, pairs)), o...]
    unnamed x2 -> x1, local copies, waits for them, and re-layouts: 4.21 us -> 2.39 us
where the time goes in v2:
time: 37.6 us; the launch traced here: 37.5 us
  Pallas kernels  35.1 us (93%)
  local copies, waits for them, and re-layouts  2.39 us (6%)
    pallas_call x1, Pallas kernels, shards(): pl.pallas_call(functools.partial(kernel, (Z, W, levels, slots, pairs)), o...  35.1 us
    unnamed x1, local copies, waits for them, and re-layouts  2.39 us

profile of v2, /device:TPU:0, one launch (start us, length us, event | category | flops | bytes accessed | tf_op | source)
XLA Modules:
  0.0 37.5 jit_solution(122838841491641026)
XLA Ops:
  0.0 35.1 %shard_map.82 = bf16[275,1930]{1,0:T(8,128)(2,1)} custom-call(s32[5]{0:T(128)} %held_far.1, s32[3]{0:T(128)} %lows_far.1, bf16[275,1930]{1,0:T(8,128)(2,1)} %state_far.1, bf16[3,137,2,137]{3,2,1,0:T(2,128)(2,1)} %bitcast.1, bf16[137,137]{1,0:T(8,128)(2,1)} %height_far.1, bf16[137]{0:T(256)(128)(2,1)} %pressure_far.1, bf16[137,137]{1,0:T(8,128)(2,1)} %thermal_far.1, ...), custom_call_target="tpu_custom_call" | custom-call | tf_op jit(solution)/shard_map/pallas_call | solution.py:625
  35.1 2.4 %copy.10 = bf16[275,1930]{1,0:T(8,128)(2,1)} copy(bf16[275,1930]{1,0:T(8,128)(2,1)} %shard_map.82) | data formatting | bytes 2123000

commit v3 on v2

v3 whole, which is shorter than its diff:
```python
import functools

import jax
import jax.numpy as jnp
from jax import lax
from jax.experimental import pallas as pl
from jax.experimental.pallas import tpu as pltpu
from jax.sharding import PartitionSpec as P

MESH = pl.DeviceIdType.MESH
LANES = 128
ROWS_TILE = 16
TABLE_ROWS = 8
NEAR_ROWS = 16
KEEP_BYTES = 24 << 20
scope = jax.named_scope


def ceil_to(value, step):
    return -(-value // step) * step


def kernel(
    size,
    held_far,
    lows_far,
    state_far,
    inverses_far,
    height_far,
    pressure_far,
    thermal_far,
    mass_far,
    out,
    held,
    lows,
    state,
    inverses,
    height_operator,
    pressure_column,
    thermal_response,
    mass_row,
    low_rows,
    info,
    far_info,
    matrices,
    rest,
    right,
    pick,
    outgoing,
    arrived,
    solved,
    returned,
    packed,
    packed_orders,
    pick_moved,
    pick_extra,
    extra_in,
    extra_out,
    total,
    row_send,
    row_recv,
    info_send,
    info_recv,
    z_send,
    z_recv,
    out_send,
    out_recv,
    back_send,
    back_recv,
    fetch_sem,
):
    Z, W, levels, slots, pairs = size
    half_count = Z * W * pairs
    truncation = 2 * half_count - 1
    slot_width = 2 * (truncation + 2)
    width = slots * slot_width
    denom = float(truncation * (truncation + 1))
    per_pair = 4 * slots
    block_pairs = 2 * pairs
    first_extra = block_pairs * per_pair
    moved = per_pair - 2
    tiles = packed.shape[2] // LANES
    last_slot = slots - 1
    tail = levels - LANES
    keep = pick.shape[1] > 1
    z = lax.axis_index("grp")
    w = lax.axis_index("wave")
    middle = jnp.logical_and(z > 0, z < Z - 1)

    barrier = pltpu.get_barrier_semaphore()

    def greet(k, carry):
        pl.semaphore_signal(
            barrier, inc=1, device_id=(z, lax.rem(w + k, W)), device_id_type=MESH
        )
        return carry

    fetches = [
        pltpu.make_async_copy(far, near, fetch_sem.at[i])
        for i, (far, near) in enumerate(
            [
                (lows_far, lows),
                (held_far, held),
                (inverses_far, inverses),
                (state_far, state),
                (height_far, height_operator),
                (pressure_far, pressure_column),
                (thermal_far, thermal_response),
                (mass_far, mass_row),
            ]
        )
    ]
    for k in range(1, Z):
        pl.semaphore_signal(barrier, inc=1, device_id=(lax.rem(z + k, Z), w), device_id_type=MESH)
    for fetch in fetches[:3]:
        fetch.start()
    lax.fori_loop(1, W, greet, 0)
    for fetch in fetches[3:]:
        fetch.start()

    lane = lax.broadcasted_iota(jnp.int32, (1, LANES), 1)
    lane_pair = lane // per_pair
    lane_member = lax.rem(lane, per_pair) // (2 * slots)
    lane_slot = lax.rem(lax.rem(lane, per_pair), 2 * slots) // 2
    lane_part = lax.rem(lane, 2)
    spare = lane >= first_extra
    table_row = lax.broadcasted_iota(jnp.int32, (TABLE_ROWS, LANES), 0)
    with scope("small_fetch"):
        fetches[0].wait()
        fetches[1].wait()
    orders = jnp.full((1, LANES), -1, jnp.int32)
    for s in range(slots):
        orders = jnp.where(lane_slot == s, held[s], orders)
    low_tile = jnp.zeros((TABLE_ROWS, LANES), jnp.int32)
    for j in range(pairs):
        low_tile = jnp.where(table_row == j, lows[j], low_tile)
    low_rows[z] = low_tile

    rows = matrices.shape[2]

    def split_inverses():
        fetches[2].wait()
        to_row = lax.broadcasted_iota(jnp.int32, (2 * rows, 2 * levels), 0)
        from_row = lax.broadcasted_iota(jnp.int32, (2 * rows, 2 * levels), 1)
        wanted = jnp.where(to_row < rows, 2 * to_row, 2 * (to_row - rows) + 1)
        split = jnp.where(wanted == from_row, 1.0, 0.0).astype(jnp.bfloat16)
        ends = []
        for j in range(pairs):
            both = jnp.dot(
                split,
                inverses[j].reshape(2 * levels, levels),
                preferred_element_type=jnp.float32,
            )
            for member in range(2):
                matrix = both[member * rows : (member + 1) * rows]
                matrices[z, 2 * j + member] = matrix.astype(jnp.bfloat16)
                ends.append(matrix[:, LANES:levels])
        rest[z, :, 0 : 2 * pairs * tail] = jnp.concatenate(ends, axis=1).astype(jnp.bfloat16)

    @pl.when(middle)
    def _():
        with scope("split"):
            split_inverses()

    with scope("barrier"):
        pl.semaphore_wait(barrier, W + Z - 2)

    def z_copy(g, c, way):
        if c < pairs:
            ref = matrices.at[g, pl.ds(2 * c, 2), :, pl.ds(0, LANES)]
        else:
            ref = rest.at[g]
        step = 1 if way == 0 else -1
        return pltpu.make_async_remote_copy(
            src_ref=ref,
            dst_ref=ref,
            send_sem=z_send.at[0 if c < pairs else 1, way],
            recv_sem=z_recv.at[g, c],
            device_id=(z + step, w),
            device_id_type=MESH,
        )

    def forward(g, c):
        @pl.when(jnp.logical_and(g <= z, z < Z - 1))
        def _():
            z_copy(g, c, 0).start()

        @pl.when(jnp.logical_and(g >= z, z > 0))
        def _():
            z_copy(g, c, 1).start()

    def group_at(t):
        g = z
        for zz in range(Z):
            by_distance = sorted(range(Z), key=lambda a: abs(a - zz))
            g = jnp.where(z == zz, by_distance[t], g)
        return g

    def relay_now(*steps):
        for t, c in steps:
            g = group_at(t)
            z_copy(g, c, 0).wait_recv()
            forward(g, c)

    def relay(*steps):
        @pl.when(middle)
        def _():
            relay_now(*steps)

    def arrive(*steps):
        @pl.when(jnp.logical_not(middle))
        def _():
            for t, c in steps:
                z_copy(group_at(t), c, 0).wait_recv()

    groups = [group_at(t) for t in range(Z)]

    def row_copy(k):
        return pltpu.make_async_remote_copy(
            src_ref=low_rows.at[z],
            dst_ref=low_rows.at[z],
            send_sem=row_send,
            recv_sem=row_recv.at[k],
            device_id=(lax.rem(z + k, Z), w),
            device_id_type=MESH,
        )

    def wait_row(g):
        pltpu.make_async_remote_copy(
            src_ref=low_rows.at[g],
            dst_ref=low_rows.at[g],
            send_sem=row_send,
            recv_sem=row_recv.at[lax.rem(z + Z - g, Z)],
            device_id=(g, w),
            device_id_type=MESH,
        ).wait_recv()

    def table_copy(table, b, k):
        return pltpu.make_async_remote_copy(
            src_ref=table.at[w],
            dst_ref=table.at[w],
            send_sem=info_send.at[b],
            recv_sem=info_recv.at[b],
            device_id=(z, lax.rem(w + k, W)),
            device_id_type=MESH,
        )

    def send_table(table, b):
        def start(k, carry):
            table_copy(table, b, k).start()
            return carry

        lax.fori_loop(1, W, start, 0)

    def all_tables(table, b):
        return pltpu.make_async_remote_copy(
            src_ref=table.at[pl.ds(0, W - 1)],
            dst_ref=table.at[pl.ds(0, W - 1)],
            send_sem=info_send.at[b],
            recv_sem=info_recv.at[b],
            device_id=(z, lax.rem(w + 1, W)),
            device_id_type=MESH,
        )

    for k in range(1, Z):
        row_copy(k).start()

    @pl.when(jnp.logical_not(middle))
    def _():
        with scope("split_end"):
            split_inverses()

    for c in [pairs, *range(pairs)]:
        forward(z, c)

    column = lax.broadcasted_iota(jnp.int32, (1, width), 1)
    column_order = jnp.full((1, width), -1, jnp.int32)
    column_start = jnp.zeros((1, width), jnp.int32)
    for s in range(slots):
        inside = jnp.logical_and(column >= s * slot_width, column < (s + 1) * slot_width)
        column_order = jnp.where(inside, held[s], column_order)
        column_start = jnp.where(inside, s * slot_width, column_start)

    def drive_right():
        coefficient = (column - column_start) // 2
        degree = jnp.where(
            coefficient <= truncation - column_order, column_order + coefficient, coefficient - 1
        )
        lap_scale = (degree * (degree + 1)).astype(jnp.float32) / denom
        fetches[4].wait()
        fetches[5].wait()
        height = height_operator[...].astype(jnp.float32)
        pressure_row = jnp.broadcast_to(
            pressure_column[...].astype(jnp.float32).reshape(1, levels), height.shape
        )
        across = lax.broadcasted_iota(jnp.int32, height.shape, 1)
        down = lax.broadcasted_iota(jnp.int32, height.shape, 0)
        pressure_side = jnp.sum(
            jnp.where(across == down, pressure_row, 0.0), axis=1, keepdims=True
        )
        height = jnp.concatenate(
            [jnp.zeros((levels, tail), jnp.float32), height, pressure_side], axis=1
        ).astype(jnp.bfloat16)
        fetches[3].wait()
        drive = jnp.dot(height, state[LANES:, :], preferred_element_type=jnp.float32)
        right[0:levels, :] = (
            state[0:levels, :].astype(jnp.float32) + lap_scale * drive
        ).astype(jnp.bfloat16)

    with scope("drive"):
        drive_right()
    with scope("rows_wait"):
        for t in range(1, 3):
            wait_row(groups[t])
    table = [low_rows[groups[t]][0:pairs] for t in range(3)]
    table += [jnp.broadcast_to(orders, (NEAR_ROWS - 3 * pairs, LANES))]
    info[w] = jnp.concatenate(table, axis=0)
    send_table(info, 0)
    with scope("row_far"):
        wait_row(groups[3])
    far_info[w] = low_rows[groups[3]]
    send_table(far_info, 1)

    @pl.when(middle)
    def _():
        with scope("relay_a"):
            relay_now((1, pairs), (2, pairs), (1, 0), (2, 0))

    with scope("info_wait"):
        all_tables(info, 0).wait_recv()

    def low_of(d, t, j):
        if t < 3:
            return info[d][t * pairs + j : t * pairs + j + 1]
        return far_info[d][j : j + 1]

    def target_of(b, k):
        d = lax.rem(w + k, W)
        pair = lax.rem(lane_pair + block_pairs - lax.rem(k, block_pairs), block_pairs)
        low = jnp.zeros((1, LANES), jnp.int32)
        for p in range(block_pairs):
            low = jnp.where(pair == p, low_of(d, 2 * b + p // pairs, p % pairs), low)
        slot, member, order = lane_slot, lane_member, orders
        if b == 0:
            low = jnp.where(spare, low_of(d, 2, 0), low)
            slot = jnp.where(spare, last_slot, slot)
            member = jnp.where(spare, 1, member)
            order = jnp.where(spare, held[last_slot], order)
        merged = jnp.where(order <= low, low - order, truncation + 1 - low)
        position = jnp.where(member == 0, merged, truncation - low - order)
        used = order >= 0
        if b == 0:
            used = jnp.logical_and(used, lane < first_extra + 2)
        else:
            hole = jnp.logical_and(pair == 0, lax.rem(lane, per_pair) >= moved)
            extra = jnp.logical_or(spare, hole)
            position = jnp.where(extra, truncation + 1 - order, position)
        target = slot * slot_width + 2 * position + lane_part
        return jnp.where(used, target, -1)

    def build(b, i, place):
        at = lax.broadcasted_iota(jnp.int32, (width, LANES), 0)
        for h in range(2):
            pick[b, place, :, h * LANES : (h + 1) * LANES] = jnp.where(
                at == target_of(b, 2 * i + h), 1.0, 0.0
            ).astype(jnp.bfloat16)

    def place_of(i):
        return i if keep else 0

    def out_copy(b, k):
        return pltpu.make_async_remote_copy(
            src_ref=outgoing.at[b, k],
            dst_ref=arrived.at[b, k],
            send_sem=out_send.at[b],
            recv_sem=out_recv.at[b],
            device_id=(z, lax.rem(w + k, W)),
            device_id_type=MESH,
        )

    def back_copy(b, k):
        return pltpu.make_async_remote_copy(
            src_ref=solved.at[b, k],
            dst_ref=returned.at[b, k],
            send_sem=back_send.at[b],
            recv_sem=back_recv.at[b, k // 2],
            device_id=(z, lax.rem(w + W - k, W)),
            device_id_type=MESH,
        )

    def send_block(b):
        def send(i, carry):
            build(b, i, place_of(i))
            message = jnp.dot(
                right[...], pick[b, place_of(i)], preferred_element_type=jnp.float32
            ).astype(jnp.bfloat16)
            k0, k1 = 2 * i, 2 * i + 1
            outgoing[b, k0] = message[:, :LANES]
            outgoing[b, k1] = message[:, LANES:]

            @pl.when(i > 0)
            def _():
                out_copy(b, k0).start()

            out_copy(b, k1).start()
            return carry

        lax.fori_loop(0, W // 2, send, 0)
        arrived[b, 0] = outgoing[b, 0]

    def all_out(b):
        return pltpu.make_async_remote_copy(
            src_ref=outgoing.at[b, pl.ds(1, W - 1)],
            dst_ref=arrived.at[b, pl.ds(1, W - 1)],
            send_sem=out_send.at[b],
            recv_sem=out_recv.at[b],
            device_id=(z, lax.rem(w + 1, W)),
            device_id_type=MESH,
        )

    def some_back(b, first, count):
        return pltpu.make_async_remote_copy(
            src_ref=solved.at[b, pl.ds(first, count)],
            dst_ref=returned.at[b, pl.ds(first, count)],
            send_sem=back_send.at[b],
            recv_sem=back_recv.at[b, first // 2],
            device_id=(z, lax.rem(w + 1, W)),
            device_id_type=MESH,
        )

    with scope("send0"):
        send_block(0)
    with scope("relay_b"):
        for c in range(1, pairs):
            relay((1, c), (2, c))
    with scope("far_wait"):
        all_tables(far_info, 1).wait_recv()
    with scope("send1"):
        send_block(1)
    with scope("relay_c"):
        relay((3, pairs), (3, 0))

    def fill_rest(t):
        g = groups[t]
        for i in range(2 * pairs):
            piece = rest[g].astype(jnp.float32)[:, i * tail : (i + 1) * tail]
            matrices[g, i, :, LANES:levels] = piece.astype(jnp.bfloat16)

    def spread(row):
        return jnp.concatenate([row] * tiles, axis=1)

    source_orders = [
        info[lax.rem(w + W - k, W)][3 * pairs : 3 * pairs + 1] for k in range(W)
    ]

    def place(p, k):
        return lane_pair == (p + k) % block_pairs

    def pack(b, p):
        for v in range(tiles):
            first = v * block_pairs
            columns = arrived[b, first, 0:levels, :]
            order = source_orders[first]
            for k in range(first + 1, min(first + block_pairs, W)):
                columns = jnp.where(place(p, k), arrived[b, k, 0:levels, :], columns)
                order = jnp.where(place(p, k), source_orders[k], order)
            part = slice(v * LANES, (v + 1) * LANES)
            packed[b * block_pairs + p, 0:levels, part] = columns
            if b == 0:
                packed_orders[p : p + 1, part] = order

    wide_member = spread(lane_member)

    def times(t, j, member, x):
        return jnp.dot(
            matrices[groups[t], 2 * j + member], x, preferred_element_type=jnp.float32
        )

    def solve(b, p):
        t, j = 2 * b + p // pairs, p % pairs
        x = packed[b * block_pairs + p, 0:levels, :]
        low = spread(low_of(w, t, j))
        use_low = jnp.logical_and(wide_member == 0, packed_orders[p : p + 1, :] <= low)
        y = jnp.where(use_low, times(t, j, 0, x), times(t, j, 1, x))
        return y.astype(jnp.bfloat16)

    def deal(b, ps, answers, fresh):
        for k in range(W):
            v = k // block_pairs
            parts = [y[:, v * LANES : (v + 1) * LANES] for y in answers]
            block = parts[0] if fresh else solved[b, k]
            for p, part in list(zip(ps, parts))[1 if fresh else 0 :]:
                block = jnp.where(place(p, k), part, block)
            solved[b, k] = block

    def start_back(b):
        for k in range(1, W):
            back_copy(b, k).start()

    def gather_spare(b, chosen):
        columns = jnp.concatenate([arrived[b, k, 0:levels, :] for k in range(W)], axis=1)
        return jnp.dot(columns, chosen[...], preferred_element_type=jnp.float32).astype(
            jnp.bfloat16
        )

    def scatter_spare(b, answer, chosen, where):
        back = lax.dot_general(
            answer, chosen[...], (((1,), (1,)), ((), ())), preferred_element_type=jnp.float32
        ).astype(jnp.bfloat16)
        for k in range(W):
            part = back[:, k * LANES : (k + 1) * LANES]
            solved[b, k] = jnp.where(where(k), part, solved[b, k])

    def is_extra(k):
        start = per_pair * (k % block_pairs) + moved
        return jnp.logical_or(spare, jnp.logical_and(lane >= start, lane < start + 2))

    def choose():
        for b, ref in ((0, pick_moved), (1, pick_extra)):
            row = lax.broadcasted_iota(jnp.int32, ref.shape, 0)
            at = lax.broadcasted_iota(jnp.int32, ref.shape, 1)
            k, own = row // LANES, lax.rem(row, LANES)
            if b == 0:
                wanted = 2 * k + own - first_extra
                valid = jnp.logical_and(own >= first_extra, own < first_extra + 2)
            else:
                start = per_pair * lax.rem(k, block_pairs) + moved
                hole = jnp.logical_and(own >= start, own < start + 2)
                last = 2 * last_slot + own - start
                wanted = 2 * slots * k + jnp.where(hole, last, own - first_extra)
                valid = jnp.logical_or(hole, own >= first_extra)
            ref[...] = jnp.where(jnp.logical_and(valid, at == wanted), 1.0, 0.0).astype(
                jnp.bfloat16
            )

    extra_width = extra_in.shape[1]

    def along(row):
        return jnp.concatenate([row] * (extra_width // LANES), axis=1)

    extra_lane = lax.broadcasted_iota(jnp.int32, (1, extra_width), 1)
    extra_slot = lax.rem(extra_lane, 2 * slots) // 2
    extra_order = jnp.full((1, extra_width), -1, jnp.int32)
    for k in range(W):
        for s in range(slots):
            here = jnp.logical_and(extra_lane // (2 * slots) == k, extra_slot == s)
            value = source_orders[k][:, 2 * s : 2 * s + 1]
            extra_order = jnp.where(here, value, extra_order)

    def solve_extra(steps):
        x = extra_in[0:levels, :]
        y = extra_out[...]
        for t, j in steps:
            hit = extra_order == along(low_of(w, t, j))
            y = jnp.where(hit, times(t, j, 1, x).astype(jnp.bfloat16), y)
        extra_out[...] = y

    def late(ps):
        deal(1, ps, [solve(1, p) for p in ps], False)
        solve_extra([(2 + p // pairs, p % pairs) for p in ps])

    with scope("choose"):
        choose()
    with scope("wait0"):
        all_out(0).wait_recv()
    with scope("pack0"):
        for p in range(block_pairs):
            pack(0, p)
    with scope("moved"):
        moved_in = gather_spare(0, pick_moved)
    with scope("arrive1"):
        arrive((1, pairs), *[(1, c) for c in range(pairs)])
    fill_rest(1)
    with scope("near"):
        every = list(range(block_pairs))
        deal(0, every, [solve(0, p) for p in every], True)
    with scope("arrive2"):
        relay(*[(3, c) for c in range(1, pairs)])
        arrive((2, pairs), (2, 0))
    fill_rest(2)
    with scope("moved_back"):
        answer = times(2, 0, 1, moved_in).astype(jnp.bfloat16)
        scatter_spare(0, answer, pick_moved, lambda k: spare)
        start_back(0)
    with scope("wait1"):
        all_out(1).wait_recv()
    with scope("pack1"):
        for p in range(block_pairs):
            pack(1, p)
        extra_in[0:levels, :] = gather_spare(1, pick_extra)
        extra_out[...] = jnp.zeros_like(extra_out)
    with scope("extra"):
        solve_extra([(t, j) for t in range(2) for j in range(pairs)])
    with scope("late2a"):
        deal(1, [0], [solve(1, 0)], True)
        solve_extra([(2, 0)])
    with scope("arrive2b"):
        arrive(*[(2, c) for c in range(1, pairs)])
    with scope("late2b"):
        late(list(range(1, pairs)))
    with scope("arrive3"):
        arrive((3, pairs), *[(3, c) for c in range(pairs - 1)])
    fill_rest(3)
    with scope("late3a"):
        late(list(range(pairs, block_pairs - 1)))
    with scope("arrive3b"):
        arrive((3, pairs - 1))
    with scope("late3b"):
        late([block_pairs - 1])
        scatter_spare(1, extra_out[...], pick_extra, is_extra)
        start_back(1)

    fetches[6].wait()
    fetches[7].wait()
    total[...] = jnp.zeros_like(total)
    through_row = lax.broadcasted_iota(jnp.int32, (tail, levels), 0)
    through_lane = lax.broadcasted_iota(jnp.int32, (tail, levels), 1)
    response = jnp.concatenate(
        [
            jnp.where(through_lane == through_row + LANES, -1.0, 0.0),
            thermal_response[...].astype(jnp.float32),
            mass_row[...].astype(jnp.float32).reshape(1, levels),
        ],
        axis=0,
    ).astype(jnp.bfloat16)

    def collect(b, i, first, second):
        if not keep:
            build(b, i, 0)
        total[...] += lax.dot_general(
            jnp.concatenate([first, second], axis=1),
            pick[b, place_of(i)],
            (((1,), (1,)), ((), ())),
            preferred_element_type=jnp.float32,
        )

    def gather_back(b):
        with scope(f"back{b}_0"):
            some_back(b, 1, 1).wait_recv()
            collect(b, 0, solved[b, 0], returned[b, 1])

        def step(i, carry):
            some_back(b, 2 * i, 2).wait_recv()
            collect(b, i, returned[b, 2 * i], returned[b, 2 * i + 1])
            return carry

        with scope(f"back{b}"):
            lax.fori_loop(1, W // 2, step, 0)

    gather_back(0)
    gather_back(1)

    with scope("final"):
        div = total[0:levels, :].astype(jnp.bfloat16)
        change = jnp.dot(response, div, preferred_element_type=jnp.float32)
        old = state[LANES:, :].astype(jnp.float32)
        below = lax.broadcasted_iota(jnp.int32, old.shape, 0) < tail
        new = jnp.where(below, 0.0, old) - change
        new = jnp.where(column_order >= 0, new, 0.0)
        out[0:LANES, :] = div[0:LANES, :]
        out[LANES:, :] = new.astype(jnp.bfloat16)

    for b, table in ((0, info), (1, far_info)):
        all_out(b).wait_send()
        pltpu.make_async_remote_copy(
            src_ref=solved.at[b, pl.ds(1, W - 1)],
            dst_ref=returned.at[b, pl.ds(1, W - 1)],
            send_sem=back_send.at[b],
            recv_sem=back_recv.at[b, 0],
            device_id=(z, lax.rem(w + 1, W)),
            device_id_type=MESH,
        ).wait_send()
        all_tables(table, b).wait_send()
    pltpu.make_async_remote_copy(
        src_ref=low_rows.at[pl.ds(0, Z - 1)],
        dst_ref=low_rows.at[pl.ds(0, Z - 1)],
        send_sem=row_send,
        recv_sem=row_recv.at[1],
        device_id=(lax.rem(z + 1, Z), w),
        device_id_type=MESH,
    ).wait_send()

    def wait_relayed(count, way):
        for kind, ref in (
            (0, matrices.at[pl.ds(0, count), :, :, pl.ds(0, LANES)]),
            (1, rest.at[pl.ds(0, count)]),
        ):
            pltpu.make_async_remote_copy(
                src_ref=ref,
                dst_ref=ref,
                send_sem=z_send.at[kind, way],
                recv_sem=z_recv.at[0, 0],
                device_id=(lax.rem(z + 1, Z), w),
                device_id_type=MESH,
            ).wait_send()

    for zz in range(Z):

        @pl.when(z == zz)
        def _():
            if zz < Z - 1:
                wait_relayed(zz + 1, 0)
            if zz > 0:
                wait_relayed(Z - zz, 1)


def shards(
    state,
    held_orders,
    pair_lows,
    inverses,
    height_operator,
    pressure_column,
    thermal_response_matrix,
    mass_row,
):
    levels = height_operator.shape[0]
    slots = held_orders.shape[0]
    pairs = pair_lows.shape[0]
    Z, W = lax.axis_size("grp"), lax.axis_size("wave")
    width = state.shape[1]
    rows = ceil_to(levels, ROWS_TILE)
    places = W // 2 if W * width * 4 * LANES <= KEEP_BYTES else 1
    tiles = -(-W // (2 * pairs))
    extra_width = ceil_to(2 * slots * W, LANES)
    block = pltpu.VMEM((2, W, rows, LANES), jnp.bfloat16)
    return pl.pallas_call(
        functools.partial(kernel, (Z, W, levels, slots, pairs)),
        out_shape=pltpu.VMEM(state.shape, jnp.bfloat16),
        in_specs=[pl.BlockSpec(memory_space=pl.ANY)] * 8,
        out_specs=pl.BlockSpec(memory_space=pltpu.VMEM),
        scratch_shapes=[
            pltpu.SMEM(held_orders.shape, jnp.int32),
            pltpu.SMEM(pair_lows.shape, jnp.int32),
            pltpu.VMEM(state.shape, jnp.bfloat16),
            pltpu.VMEM((pairs, levels, 2, levels), jnp.bfloat16),
            pltpu.VMEM(height_operator.shape, jnp.bfloat16),
            pltpu.VMEM(pressure_column.shape, jnp.bfloat16),
            pltpu.VMEM(thermal_response_matrix.shape, jnp.bfloat16),
            pltpu.VMEM(mass_row.shape, jnp.bfloat16),
            pltpu.VMEM((Z, TABLE_ROWS, LANES), jnp.int32),
            pltpu.VMEM((W, NEAR_ROWS, LANES), jnp.int32),
            pltpu.VMEM((W, TABLE_ROWS, LANES), jnp.int32),
            pltpu.VMEM((Z, 2 * pairs, rows, levels), jnp.bfloat16),
            pltpu.VMEM((Z, rows, LANES), jnp.bfloat16),
            pltpu.VMEM((rows, width), jnp.bfloat16),
            pltpu.VMEM((2, places, width, 2 * LANES), jnp.bfloat16),
            block,
            block,
            block,
            block,
            pltpu.VMEM((4 * pairs, rows, tiles * LANES), jnp.bfloat16),
            pltpu.VMEM((ceil_to(2 * pairs, TABLE_ROWS), tiles * LANES), jnp.int32),
            pltpu.VMEM((W * LANES, ceil_to(2 * W, LANES)), jnp.bfloat16),
            pltpu.VMEM((W * LANES, extra_width), jnp.bfloat16),
            pltpu.VMEM((rows, extra_width), jnp.bfloat16),
            pltpu.VMEM((rows, extra_width), jnp.bfloat16),
            pltpu.VMEM((rows, width), jnp.float32),
            pltpu.SemaphoreType.DMA,
            pltpu.SemaphoreType.DMA((Z,)),
            pltpu.SemaphoreType.DMA((2,)),
            pltpu.SemaphoreType.DMA((2,)),
            pltpu.SemaphoreType.DMA((2, 2)),
            pltpu.SemaphoreType.DMA((Z, pairs + 1)),
            pltpu.SemaphoreType.DMA((2,)),
            pltpu.SemaphoreType.DMA((2,)),
            pltpu.SemaphoreType.DMA((2,)),
            pltpu.SemaphoreType.DMA((2, W // 2)),
            pltpu.SemaphoreType.DMA((8,)),
        ],
        compiler_params=pltpu.CompilerParams(
            collective_id=0, has_side_effects=True, vmem_limit_bytes=52 * 1024 * 1024
        ),
    )(
        *[
            pltpu.with_memory_space_constraint(array, pltpu.HBM)
            for array in (
                held_orders,
                pair_lows,
                state,
                jnp.transpose(inverses, (0, 2, 1, 3)),
                height_operator,
                pressure_column,
                thermal_response_matrix,
                mass_row,
            )
        ]
    )


def solution(mesh):
    placed = (
        P(None, ("grp", "wave")),
        P(("grp", "wave")),
        P(("grp", "wave")),
        P(("grp", "wave"), None, None, None),
        P(),
        P(),
        P(),
        P(),
    )
    return jax.shard_map(
        shards, mesh=mesh, in_specs=placed, out_specs=P(None, ("grp", "wave")), check_vma=False
    )
```

time: 37.6 us -> 33.1 us (0.88)
  Pallas kernels: 35.1 us -> 32 us
  local copies, waits for them, and re-layouts: 2.39 us -> 1 us
    pallas_call x1, Pallas kernels: 35.1 us -> 32 us  [shards(): pl.pallas_call(functools.partial(kernel, (Z, W, levels, slots, pairs)), o...]
    unnamed x1, local copies, waits for them, and re-layouts: 2.39 us -> 1 us
where the time goes in v3:
time: 33.1 us; the launch traced here: 33 us
  Pallas kernels  32 us (97%)
  local copies, waits for them, and re-layouts  1 us (3%)
    pallas_call x1, Pallas kernels, shards(): pl.pallas_call(functools.partial(kernel, (Z, W, levels, slots, pairs)), o...  32 us
    unnamed x1, local copies, waits for them, and re-layouts  1 us

profile of v3, /device:TPU:0, one launch (start us, length us, event | category | flops | bytes accessed | tf_op | source)
XLA Modules:
  0.0 33.0 jit_solution(1487410784968493965)
XLA Ops:
  0.0 32.0 %shard_map.82 = bf16[275,1930]{1,0:T(8,128)(2,1)S(1)} custom-call(s32[5]{0:T(128)} %held_far.1, s32[3]{0:T(128)} %lows_far.1, bf16[275,1930]{1,0:T(8,128)(2,1)} %state_far.1, bf16[3,137,2,137]{3,2,1,0:T(2,128)(2,1)} %bitcast.1, bf16[137,137]{1,0:T(8,128)(2,1)} %height_far.1, bf16[137]{0:T(256)(128)(2,1)} %pressure_far.1, bf16[137,137]{1,0:T(8,128)(2,1)} %thermal_far.1, ...), custom_call_target="tpu_custom_call" | custom-call | tf_op jit(solution)/shard_map/pallas_call | solution.py:727
  32.0 1.0 %copy.10 = bf16[275,1930]{1,0:T(8,128)(2,1)} copy(bf16[275,1930]{1,0:T(8,128)(2,1)S(1)} %shard_map.82) | data formatting | bytes 2123000

commit v4 on v3

--- a/solution.py
+++ b/solution.py
@@ -43,7 +43,7 @@
     info,
     far_info,
     matrices,
-    rest,
+    edges,
     right,
     pick,
     outgoing,
@@ -82,6 +82,7 @@
     tiles = packed.shape[2] // LANES
     last_slot = slots - 1
     tail = levels - LANES
+    border = 2 * pairs * tail
     keep = pick.shape[1] > 1
     z = lax.axis_index("grp")
     w = lax.axis_index("wave")
@@ -144,7 +145,7 @@
         from_row = lax.broadcasted_iota(jnp.int32, (2 * rows, 2 * levels), 1)
         wanted = jnp.where(to_row < rows, 2 * to_row, 2 * (to_row - rows) + 1)
         split = jnp.where(wanted == from_row, 1.0, 0.0).astype(jnp.bfloat16)
-        ends = []
+        parts = []
         for j in range(pairs):
             both = jnp.dot(
                 split,
@@ -154,10 +155,17 @@
             for member in range(2):
                 matrix = both[member * rows : (member + 1) * rows]
                 matrices[z, 2 * j + member] = matrix.astype(jnp.bfloat16)
-                ends.append(matrix[:, LANES:levels])
-        rest[z, :, 0 : 2 * pairs * tail] = jnp.concatenate(ends, axis=1).astype(jnp.bfloat16)
-
-    @pl.when(middle)
+                parts.append(matrix)
+        blank = jnp.zeros((LANES, LANES - border), jnp.float32)
+        under = [matrix[LANES:levels, 0:LANES] for matrix in parts]
+        aside = jnp.concatenate([m[0:LANES, LANES:levels] for m in parts] + [blank], axis=1)
+        corner = [m[LANES:levels, LANES:levels] for m in parts] + [blank[0:tail]]
+        corner = jnp.concatenate(corner, axis=1)
+        filler = jnp.zeros((LANES - 2 * border - tail, LANES), jnp.float32)
+        edge = jnp.concatenate([*under, aside.T[0:border], corner, filler], axis=0)
+        edges[z] = edge.astype(jnp.bfloat16)
+
+    @pl.when(z < Z - 1)
     def _():
         with scope("split"):
             split_inverses()
@@ -167,9 +175,9 @@
 
     def z_copy(g, c, way):
         if c < pairs:
-            ref = matrices.at[g, pl.ds(2 * c, 2), :, pl.ds(0, LANES)]
+            ref = matrices.at[g, pl.ds(2 * c, 2), pl.ds(0, LANES), pl.ds(0, LANES)]
         else:
-            ref = rest.at[g]
+            ref = edges.at[g]
         step = 1 if way == 0 else -1
         return pltpu.make_async_remote_copy(
             src_ref=ref,
@@ -192,7 +200,7 @@
     def group_at(t):
         g = z
         for zz in range(Z):
-            by_distance = sorted(range(Z), key=lambda a: abs(a - zz))
+            by_distance = sorted(range(Z), key=lambda a: (abs(a - zz), abs(2 * a - Z + 1)))
             g = jnp.where(z == zz, by_distance[t], g)
         return g
 
@@ -265,7 +273,7 @@
     for k in range(1, Z):
         row_copy(k).start()
 
-    @pl.when(jnp.logical_not(middle))
+    @pl.when(z == Z - 1)
     def _():
         with scope("split_end"):
             split_inverses()
@@ -324,7 +332,7 @@
     @pl.when(middle)
     def _():
         with scope("relay_a"):
-            relay_now((1, pairs), (2, pairs), (1, 0), (2, 0))
+            relay_now((1, pairs), (1, 0), (2, pairs), (2, 0), (1, 1))
 
     with scope("info_wait"):
         all_tables(info, 0).wait_recv()
@@ -388,7 +396,7 @@
             device_id_type=MESH,
         )
 
-    def send_block(b):
+    def send_block(b, start, stop):
         def send(i, carry):
             build(b, i, place_of(i))
             message = jnp.dot(
@@ -405,8 +413,7 @@
             out_copy(b, k1).start()
             return carry
 
-        lax.fori_loop(0, W // 2, send, 0)
-        arrived[b, 0] = outgoing[b, 0]
+        lax.fori_loop(start, stop, send, 0)
 
     def all_out(b):
         return pltpu.make_async_remote_copy(
@@ -429,22 +436,39 @@
         )
 
     with scope("send0"):
-        send_block(0)
+        send_block(0, 0, W // 4)
     with scope("relay_b"):
-        for c in range(1, pairs):
-            relay((1, c), (2, c))
+        relay((1, 2), (2, 1))
+    with scope("send0b"):
+        send_block(0, W // 4, W // 2)
+    with scope("relay_c"):
+        relay((2, 2), (3, pairs))
     with scope("far_wait"):
         all_tables(far_info, 1).wait_recv()
     with scope("send1"):
-        send_block(1)
-    with scope("relay_c"):
-        relay((3, pairs), (3, 0))
-
-    def fill_rest(t):
+        send_block(1, 0, W // 4)
+    with scope("relay_d"):
+        relay((3, 0))
+    with scope("send1b"):
+        send_block(1, W // 4, W // 2)
+    with scope("relay_e"):
+        relay((3, 1))
+    for b in range(2):
+        arrived[b, 0] = outgoing[b, 0]
+
+    def fill_edges(t):
         g = groups[t]
+        edge = edges[g].astype(jnp.float32)
+        across = edge.T
         for i in range(2 * pairs):
-            piece = rest[g].astype(jnp.float32)[:, i * tail : (i + 1) * tail]
-            matrices[g, i, :, LANES:levels] = piece.astype(jnp.bfloat16)
+            at = i * tail
+            side = across[:, border + at : border + at + tail]
+            below = jnp.concatenate(
+                [edge[at : at + tail], edge[2 * border : 2 * border + tail, at : at + tail]],
+                axis=1,
+            )
+            matrices[g, i, 0:LANES, LANES:levels] = side.astype(jnp.bfloat16)
+            matrices[g, i, LANES:levels, :] = below.astype(jnp.bfloat16)
 
     def spread(row):
         return jnp.concatenate([row] * tiles, axis=1)
@@ -570,14 +594,14 @@
         moved_in = gather_spare(0, pick_moved)
     with scope("arrive1"):
         arrive((1, pairs), *[(1, c) for c in range(pairs)])
-    fill_rest(1)
+    fill_edges(1)
     with scope("near"):
         every = list(range(block_pairs))
         deal(0, every, [solve(0, p) for p in every], True)
     with scope("arrive2"):
-        relay(*[(3, c) for c in range(1, pairs)])
+        relay((3, 2))
         arrive((2, pairs), (2, 0))
-    fill_rest(2)
+    fill_edges(2)
     with scope("moved_back"):
         answer = times(2, 0, 1, moved_in).astype(jnp.bfloat16)
         scatter_spare(0, answer, pick_moved, lambda k: spare)
@@ -600,7 +624,7 @@
         late(list(range(1, pairs)))
     with scope("arrive3"):
         arrive((3, pairs), *[(3, c) for c in range(pairs - 1)])
-    fill_rest(3)
+    fill_edges(3)
     with scope("late3a"):
         late(list(range(pairs, block_pairs - 1)))
     with scope("arrive3b"):
@@ -682,8 +706,8 @@
 
     def wait_relayed(count, way):
         for kind, ref in (
-            (0, matrices.at[pl.ds(0, count), :, :, pl.ds(0, LANES)]),
-            (1, rest.at[pl.ds(0, count)]),
+            (0, matrices.at[pl.ds(0, count), :, pl.ds(0, LANES), pl.ds(0, LANES)]),
+            (1, edges.at[pl.ds(0, count)]),
         ):
             pltpu.make_async_remote_copy(
                 src_ref=ref,
@@ -742,7 +766,7 @@
             pltpu.VMEM((W, NEAR_ROWS, LANES), jnp.int32),
             pltpu.VMEM((W, TABLE_ROWS, LANES), jnp.int32),
             pltpu.VMEM((Z, 2 * pairs, rows, levels), jnp.bfloat16),
-            pltpu.VMEM((Z, rows, LANES), jnp.bfloat16),
+            pltpu.VMEM((Z, LANES, LANES), jnp.bfloat16),
             pltpu.VMEM((rows, width), jnp.bfloat16),
             pltpu.VMEM((2, places, width, 2 * LANES), jnp.bfloat16),
             block,

time: 33.1 us -> 31.5 us (0.952)
  Pallas kernels: 32 us -> 30.3 us
    pallas_call x1, Pallas kernels: 32 us -> 30.3 us  [shards(): pl.pallas_call(functools.partial(kernel, (Z, W, levels, slots, pairs)), o...]
where the time goes in v4:
time: 31.5 us; the launch traced here: 31.3 us
  Pallas kernels  30.3 us (96%)
  local copies, waits for them, and re-layouts  1 us (3%)
    pallas_call x1, Pallas kernels, shards(): pl.pallas_call(functools.partial(kernel, (Z, W, levels, slots, pairs)), o...  30.3 us
    unnamed x1, local copies, waits for them, and re-layouts  1 us

profile of v4, /device:TPU:0, one launch (start us, length us, event | category | flops | bytes accessed | tf_op | source)
XLA Modules:
  0.0 31.3 jit_solution(9356249763476122638)
XLA Ops:
  0.0 30.3 %shard_map.82 = bf16[275,1930]{1,0:T(8,128)(2,1)S(1)} custom-call(s32[5]{0:T(128)} %held_far.1, s32[3]{0:T(128)} %lows_far.1, bf16[275,1930]{1,0:T(8,128)(2,1)} %state_far.1, bf16[3,137,2,137]{3,2,1,0:T(2,128)(2,1)} %bitcast.1, bf16[137,137]{1,0:T(8,128)(2,1)} %height_far.1, bf16[137]{0:T(256)(128)(2,1)} %pressure_far.1, bf16[137,137]{1,0:T(8,128)(2,1)} %thermal_far.1, ...), custom_call_target="tpu_custom_call" | custom-call | tf_op jit(solution)/shard_map/pallas_call | solution.py:751
  30.3 1.0 %copy.10 = bf16[275,1930]{1,0:T(8,128)(2,1)} copy(bf16[275,1930]{1,0:T(8,128)(2,1)S(1)} %shard_map.82) | data formatting | bytes 2123000

commit v5 on v4

--- a/solution.py
+++ b/solution.py
@@ -52,7 +52,6 @@
     returned,
     packed,
     packed_orders,
-    pick_moved,
     pick_extra,
     extra_in,
     extra_out,
@@ -90,10 +89,15 @@
 
     barrier = pltpu.get_barrier_semaphore()
 
+    def peer(k):
+        other = 0
+        for i in range(W.bit_length() - 1):
+            mine, flip = lax.rem(w // (1 << i), 2), lax.rem(k // (1 << i), 2)
+            other = other + (1 << i) * (mine + flip - 2 * mine * flip)
+        return other
+
     def greet(k, carry):
-        pl.semaphore_signal(
-            barrier, inc=1, device_id=(z, lax.rem(w + k, W)), device_id_type=MESH
-        )
+        pl.semaphore_signal(barrier, inc=1, device_id=(z, peer(k)), device_id_type=MESH)
         return carry
 
     fetches = [
@@ -223,22 +227,29 @@
 
     groups = [group_at(t) for t in range(Z)]
 
-    def row_copy(k):
+    def row_copy(g):
         return pltpu.make_async_remote_copy(
             src_ref=low_rows.at[z],
             dst_ref=low_rows.at[z],
             send_sem=row_send,
-            recv_sem=row_recv.at[k],
-            device_id=(lax.rem(z + k, Z), w),
-            device_id_type=MESH,
-        )
+            recv_sem=row_recv.at[z],
+            device_id=(g, w),
+            device_id_type=MESH,
+        )
+
+    def send_rows(distance):
+        for step in (-distance, distance):
+
+            @pl.when(jnp.logical_and(z + step >= 0, z + step < Z))
+            def _():
+                row_copy(z + step).start()
 
     def wait_row(g):
         pltpu.make_async_remote_copy(
             src_ref=low_rows.at[g],
             dst_ref=low_rows.at[g],
             send_sem=row_send,
-            recv_sem=row_recv.at[lax.rem(z + Z - g, Z)],
+            recv_sem=row_recv.at[g],
             device_id=(g, w),
             device_id_type=MESH,
         ).wait_recv()
@@ -249,13 +260,13 @@
             dst_ref=table.at[w],
             send_sem=info_send.at[b],
             recv_sem=info_recv.at[b],
-            device_id=(z, lax.rem(w + k, W)),
+            device_id=(z, peer(k)),
             device_id_type=MESH,
         )
 
     def send_table(table, b):
-        def start(k, carry):
-            table_copy(table, b, k).start()
+        def start(n, carry):
+            table_copy(table, b, W - n).start()
             return carry
 
         lax.fori_loop(1, W, start, 0)
@@ -266,12 +277,12 @@
             dst_ref=table.at[pl.ds(0, W - 1)],
             send_sem=info_send.at[b],
             recv_sem=info_recv.at[b],
-            device_id=(z, lax.rem(w + 1, W)),
-            device_id_type=MESH,
-        )
-
-    for k in range(1, Z):
-        row_copy(k).start()
+            device_id=(z, peer(1)),
+            device_id_type=MESH,
+        )
+
+    for distance in range(1, Z):
+        send_rows(distance)
 
     @pl.when(z == Z - 1)
     def _():
@@ -288,6 +299,19 @@
         inside = jnp.logical_and(column >= s * slot_width, column < (s + 1) * slot_width)
         column_order = jnp.where(inside, held[s], column_order)
         column_start = jnp.where(inside, s * slot_width, column_start)
+
+    def choose():
+        row = lax.broadcasted_iota(jnp.int32, pick_extra.shape, 0)
+        at = lax.broadcasted_iota(jnp.int32, pick_extra.shape, 1)
+        k, own = row // LANES, lax.rem(row, LANES)
+        start = per_pair * lax.rem(k, block_pairs) + moved
+        hole = jnp.logical_and(own >= start, own < start + 2)
+        last = 2 * last_slot + own - start
+        wanted = 2 * slots * k + jnp.where(hole, last, own - first_extra)
+        valid = jnp.logical_or(hole, own >= first_extra)
+        pick_extra[...] = jnp.where(jnp.logical_and(valid, at == wanted), 1.0, 0.0).astype(
+            jnp.bfloat16
+        )
 
     def drive_right():
         coefficient = (column - column_start) // 2
@@ -317,6 +341,7 @@
 
     with scope("drive"):
         drive_right()
+    choose()
     with scope("rows_wait"):
         for t in range(1, 3):
             wait_row(groups[t])
@@ -343,7 +368,7 @@
         return far_info[d][j : j + 1]
 
     def target_of(b, k):
-        d = lax.rem(w + k, W)
+        d = peer(k)
         pair = lax.rem(lane_pair + block_pairs - lax.rem(k, block_pairs), block_pairs)
         low = jnp.zeros((1, LANES), jnp.int32)
         for p in range(block_pairs):
@@ -382,7 +407,7 @@
             dst_ref=arrived.at[b, k],
             send_sem=out_send.at[b],
             recv_sem=out_recv.at[b],
-            device_id=(z, lax.rem(w + k, W)),
+            device_id=(z, peer(k)),
             device_id_type=MESH,
         )
 
@@ -392,12 +417,13 @@
             dst_ref=returned.at[b, k],
             send_sem=back_send.at[b],
             recv_sem=back_recv.at[b, k // 2],
-            device_id=(z, lax.rem(w + W - k, W)),
+            device_id=(z, peer(k)),
             device_id_type=MESH,
         )
 
     def send_block(b, start, stop):
-        def send(i, carry):
+        def send(step, carry):
+            i = W // 2 - 1 - step
             build(b, i, place_of(i))
             message = jnp.dot(
                 right[...], pick[b, place_of(i)], preferred_element_type=jnp.float32
@@ -421,7 +447,7 @@
             dst_ref=arrived.at[b, pl.ds(1, W - 1)],
             send_sem=out_send.at[b],
             recv_sem=out_recv.at[b],
-            device_id=(z, lax.rem(w + 1, W)),
+            device_id=(z, peer(1)),
             device_id_type=MESH,
         )
 
@@ -431,7 +457,7 @@
             dst_ref=returned.at[b, pl.ds(first, count)],
             send_sem=back_send.at[b],
             recv_sem=back_recv.at[b, first // 2],
-            device_id=(z, lax.rem(w + 1, W)),
+            device_id=(z, peer(1)),
             device_id_type=MESH,
         )
 
@@ -474,7 +500,7 @@
         return jnp.concatenate([row] * tiles, axis=1)
 
     source_orders = [
-        info[lax.rem(w + W - k, W)][3 * pairs : 3 * pairs + 1] for k in range(W)
+        info[peer(k)][3 * pairs : 3 * pairs + 1] for k in range(W)
     ]
 
     def place(p, k):
@@ -518,7 +544,7 @@
             solved[b, k] = block
 
     def start_back(b):
-        for k in range(1, W):
+        for k in range(W - 1, 0, -1):
             back_copy(b, k).start()
 
     def gather_spare(b, chosen):
@@ -538,24 +564,6 @@
     def is_extra(k):
         start = per_pair * (k % block_pairs) + moved
         return jnp.logical_or(spare, jnp.logical_and(lane >= start, lane < start + 2))
-
-    def choose():
-        for b, ref in ((0, pick_moved), (1, pick_extra)):
-            row = lax.broadcasted_iota(jnp.int32, ref.shape, 0)
-            at = lax.broadcasted_iota(jnp.int32, ref.shape, 1)
-            k, own = row // LANES, lax.rem(row, LANES)
-            if b == 0:
-                wanted = 2 * k + own - first_extra
-                valid = jnp.logical_and(own >= first_extra, own < first_extra + 2)
-            else:
-                start = per_pair * lax.rem(k, block_pairs) + moved
-                hole = jnp.logical_and(own >= start, own < start + 2)
-                last = 2 * last_slot + own - start
-                wanted = 2 * slots * k + jnp.where(hole, last, own - first_extra)
-                valid = jnp.logical_or(hole, own >= first_extra)
-            ref[...] = jnp.where(jnp.logical_and(valid, at == wanted), 1.0, 0.0).astype(
-                jnp.bfloat16
-            )
 
     extra_width = extra_in.shape[1]
 
@@ -583,29 +591,33 @@
         deal(1, ps, [solve(1, p) for p in ps], False)
         solve_extra([(2 + p // pairs, p % pairs) for p in ps])
 
-    with scope("choose"):
-        choose()
+    with scope("arrive1"):
+        relay((3, 2))
+        arrive((1, pairs), *[(1, c) for c in range(pairs)], (2, pairs))
+    fill_edges(1)
+    fill_edges(2)
     with scope("wait0"):
         all_out(0).wait_recv()
     with scope("pack0"):
         for p in range(block_pairs):
             pack(0, p)
-    with scope("moved"):
-        moved_in = gather_spare(0, pick_moved)
-    with scope("arrive1"):
-        arrive((1, pairs), *[(1, c) for c in range(pairs)])
-    fill_edges(1)
     with scope("near"):
         every = list(range(block_pairs))
         deal(0, every, [solve(0, p) for p in every], True)
     with scope("arrive2"):
-        relay((3, 2))
-        arrive((2, pairs), (2, 0))
-    fill_edges(2)
+        arrive((2, 0))
     with scope("moved_back"):
-        answer = times(2, 0, 1, moved_in).astype(jnp.bfloat16)
-        scatter_spare(0, answer, pick_moved, lambda k: spare)
-        start_back(0)
+        for k in range(W - 2, -1, -2):
+            x = [arrived[0, k + h, 0:levels, :] for h in range(2)]
+            y = times(2, 0, 1, jnp.concatenate(x, axis=1)).astype(jnp.bfloat16)
+            for h in range(2):
+                part = y[:, h * LANES : (h + 1) * LANES]
+                solved[0, k + h] = jnp.where(spare, part, solved[0, k + h])
+                if k + h > 0:
+                    back_copy(0, k + h).start()
+    with scope("edges3"):
+        arrive((3, pairs))
+        fill_edges(3)
     with scope("wait1"):
         all_out(1).wait_recv()
     with scope("pack1"):
@@ -623,8 +635,7 @@
     with scope("late2b"):
         late(list(range(1, pairs)))
     with scope("arrive3"):
-        arrive((3, pairs), *[(3, c) for c in range(pairs - 1)])
-    fill_edges(3)
+        arrive(*[(3, c) for c in range(pairs - 1)])
     with scope("late3a"):
         late(list(range(pairs, block_pairs - 1)))
     with scope("arrive3b"):
@@ -659,17 +670,17 @@
         )
 
     def gather_back(b):
+        def step(n, carry):
+            i = W // 2 - 1 - n
+            some_back(b, 2 * i, 2).wait_recv()
+            collect(b, i, returned[b, 2 * i], returned[b, 2 * i + 1])
+            return carry
+
+        with scope(f"back{b}"):
+            lax.fori_loop(0, W // 2 - 1, step, 0)
         with scope(f"back{b}_0"):
             some_back(b, 1, 1).wait_recv()
             collect(b, 0, solved[b, 0], returned[b, 1])
-
-        def step(i, carry):
-            some_back(b, 2 * i, 2).wait_recv()
-            collect(b, i, returned[b, 2 * i], returned[b, 2 * i + 1])
-            return carry
-
-        with scope(f"back{b}"):
-            lax.fori_loop(1, W // 2, step, 0)
 
     gather_back(0)
     gather_back(1)
@@ -691,7 +702,7 @@
             dst_ref=returned.at[b, pl.ds(1, W - 1)],
             send_sem=back_send.at[b],
             recv_sem=back_recv.at[b, 0],
-            device_id=(z, lax.rem(w + 1, W)),
+            device_id=(z, peer(1)),
             device_id_type=MESH,
         ).wait_send()
         all_tables(table, b).wait_send()
@@ -775,7 +786,6 @@
             block,
             pltpu.VMEM((4 * pairs, rows, tiles * LANES), jnp.bfloat16),
             pltpu.VMEM((ceil_to(2 * pairs, TABLE_ROWS), tiles * LANES), jnp.int32),
-            pltpu.VMEM((W * LANES, ceil_to(2 * W, LANES)), jnp.bfloat16),
             pltpu.VMEM((W * LANES, extra_width), jnp.bfloat16),
             pltpu.VMEM((rows, extra_width), jnp.bfloat16),
             pltpu.VMEM((rows, extra_width), jnp.bfloat16),

time: 31.5 us -> 30.7 us (0.975)
  Pallas kernels: 30.3 us -> 29.5 us
    pallas_call x1, Pallas kernels: 30.3 us -> 29.5 us  [shards(): pl.pallas_call(functools.partial(kernel, (Z, W, levels, slots, pairs)), o...]
where the time goes in v5:
time: 30.7 us; the launch traced here: 30.6 us
  Pallas kernels  29.5 us (96%)
  local copies, waits for them, and re-layouts  1 us (3%)
    pallas_call x1, Pallas kernels, shards(): pl.pallas_call(functools.partial(kernel, (Z, W, levels, slots, pairs)), o...  29.5 us
    unnamed x1, local copies, waits for them, and re-layouts  1 us

profile of v5, /device:TPU:0, one launch (start us, length us, event | category | flops | bytes accessed | tf_op | source)
XLA Modules:
  0.0 30.6 jit_solution(14477919852742986692)
XLA Ops:
  0.0 29.5 %shard_map.82 = bf16[275,1930]{1,0:T(8,128)(2,1)S(1)} custom-call(s32[5]{0:T(128)} %held_far.1, s32[3]{0:T(128)} %lows_far.1, bf16[275,1930]{1,0:T(8,128)(2,1)} %state_far.1, bf16[3,137,2,137]{3,2,1,0:T(2,128)(2,1)} %bitcast.1, bf16[137,137]{1,0:T(8,128)(2,1)} %height_far.1, bf16[137]{0:T(256)(128)(2,1)} %pressure_far.1, bf16[137,137]{1,0:T(8,128)(2,1)} %thermal_far.1, ...), custom_call_target="tpu_custom_call" | custom-call | tf_op jit(solution)/shard_map/pallas_call | solution.py:762
  29.5 1.0 %copy.10 = bf16[275,1930]{1,0:T(8,128)(2,1)} copy(bf16[275,1930]{1,0:T(8,128)(2,1)S(1)} %shard_map.82) | data formatting | bytes 2123000

commit v6 on v5

--- a/solution.py
+++ b/solution.py
@@ -12,6 +12,7 @@
 ROWS_TILE = 16
 TABLE_ROWS = 8
 NEAR_ROWS = 16
+CHUNK = 256
 KEEP_BYTES = 24 << 20
 scope = jax.named_scope
 
@@ -54,7 +55,8 @@
     packed_orders,
     pick_extra,
     extra_in,
-    extra_out,
+    put_extra,
+    last_pick,
     total,
     row_send,
     row_recv,
@@ -301,17 +303,18 @@
         column_start = jnp.where(inside, s * slot_width, column_start)
 
     def choose():
-        row = lax.broadcasted_iota(jnp.int32, pick_extra.shape, 0)
-        at = lax.broadcasted_iota(jnp.int32, pick_extra.shape, 1)
-        k, own = row // LANES, lax.rem(row, LANES)
-        start = per_pair * lax.rem(k, block_pairs) + moved
-        hole = jnp.logical_and(own >= start, own < start + 2)
-        last = 2 * last_slot + own - start
-        wanted = 2 * slots * k + jnp.where(hole, last, own - first_extra)
-        valid = jnp.logical_or(hole, own >= first_extra)
-        pick_extra[...] = jnp.where(jnp.logical_and(valid, at == wanted), 1.0, 0.0).astype(
-            jnp.bfloat16
-        )
+        for ref, dimension in ((pick_extra, 0), (put_extra, 1)):
+            row = lax.broadcasted_iota(jnp.int32, ref.shape, dimension)
+            at = lax.broadcasted_iota(jnp.int32, ref.shape, 1 - dimension)
+            k, own = row // LANES, lax.rem(row, LANES)
+            start = per_pair * lax.rem(k, block_pairs) + moved
+            hole = jnp.logical_and(own >= start, own < start + 2)
+            last = 2 * last_slot + own - start
+            wanted = 2 * slots * k + jnp.where(hole, last, own - first_extra)
+            valid = jnp.logical_or(hole, own >= first_extra)
+            ref[...] = jnp.where(jnp.logical_and(valid, at == wanted), 1.0, 0.0).astype(
+                jnp.bfloat16
+            )
 
     def drive_right():
         coefficient = (column - column_start) // 2
@@ -421,13 +424,20 @@
             device_id_type=MESH,
         )
 
-    def send_block(b, start, stop):
+    def send_block(b, first, stop):
         def send(step, carry):
             i = W // 2 - 1 - step
-            build(b, i, place_of(i))
-            message = jnp.dot(
-                right[...], pick[b, place_of(i)], preferred_element_type=jnp.float32
-            ).astype(jnp.bfloat16)
+            targets = jnp.concatenate([target_of(b, 2 * i), target_of(b, 2 * i + 1)], axis=1)
+            message = jnp.zeros((rows, 2 * LANES), jnp.float32)
+            for start in range(0, width, CHUNK):
+                count = min(CHUNK, width - start)
+                at = lax.broadcasted_iota(jnp.int32, (count, 2 * LANES), 0) + start
+                chosen = jnp.where(at == targets, 1.0, 0.0).astype(jnp.bfloat16)
+                pick[b, place_of(i), start : start + count, :] = chosen
+                message += jnp.dot(
+                    right[:, start : start + count], chosen, preferred_element_type=jnp.float32
+                )
+            message = message.astype(jnp.bfloat16)
             k0, k1 = 2 * i, 2 * i + 1
             outgoing[b, k0] = message[:, :LANES]
             outgoing[b, k1] = message[:, LANES:]
@@ -439,7 +449,7 @@
             out_copy(b, k1).start()
             return carry
 
-        lax.fori_loop(start, stop, send, 0)
+        lax.fori_loop(first, stop, send, 0)
 
     def all_out(b):
         return pltpu.make_async_remote_copy(
@@ -534,32 +544,18 @@
         y = jnp.where(use_low, times(t, j, 0, x), times(t, j, 1, x))
         return y.astype(jnp.bfloat16)
 
-    def deal(b, ps, answers, fresh):
-        for k in range(W):
-            v = k // block_pairs
-            parts = [y[:, v * LANES : (v + 1) * LANES] for y in answers]
-            block = parts[0] if fresh else solved[b, k]
-            for p, part in list(zip(ps, parts))[1 if fresh else 0 :]:
-                block = jnp.where(place(p, k), part, block)
-            solved[b, k] = block
-
-    def start_back(b):
-        for k in range(W - 1, 0, -1):
-            back_copy(b, k).start()
-
-    def gather_spare(b, chosen):
-        columns = jnp.concatenate([arrived[b, k, 0:levels, :] for k in range(W)], axis=1)
-        return jnp.dot(columns, chosen[...], preferred_element_type=jnp.float32).astype(
+    def deal(answers, k):
+        part = slice(k // block_pairs * LANES, (k // block_pairs + 1) * LANES)
+        block = answers[0][:, part]
+        for p in range(1, block_pairs):
+            block = jnp.where(place(p, k), answers[p][:, part], block)
+        return block
+
+    def gather_extra():
+        columns = jnp.concatenate([arrived[1, k, 0:levels, :] for k in range(W)], axis=1)
+        return jnp.dot(columns, pick_extra[...], preferred_element_type=jnp.float32).astype(
             jnp.bfloat16
         )
-
-    def scatter_spare(b, answer, chosen, where):
-        back = lax.dot_general(
-            answer, chosen[...], (((1,), (1,)), ((), ())), preferred_element_type=jnp.float32
-        ).astype(jnp.bfloat16)
-        for k in range(W):
-            part = back[:, k * LANES : (k + 1) * LANES]
-            solved[b, k] = jnp.where(where(k), part, solved[b, k])
 
     def is_extra(k):
         start = per_pair * (k % block_pairs) + moved
@@ -579,17 +575,12 @@
             value = source_orders[k][:, 2 * s : 2 * s + 1]
             extra_order = jnp.where(here, value, extra_order)
 
-    def solve_extra(steps):
+    def solve_extra(y, steps):
         x = extra_in[0:levels, :]
-        y = extra_out[...]
         for t, j in steps:
             hit = extra_order == along(low_of(w, t, j))
             y = jnp.where(hit, times(t, j, 1, x).astype(jnp.bfloat16), y)
-        extra_out[...] = y
-
-    def late(ps):
-        deal(1, ps, [solve(1, p) for p in ps], False)
-        solve_extra([(2 + p // pairs, p % pairs) for p in ps])
+        return y
 
     with scope("arrive1"):
         relay((3, 2))
@@ -602,8 +593,9 @@
         for p in range(block_pairs):
             pack(0, p)
     with scope("near"):
-        every = list(range(block_pairs))
-        deal(0, every, [solve(0, p) for p in every], True)
+        answers = [solve(0, p) for p in range(block_pairs)]
+        for k in range(W):
+            solved[0, k] = deal(answers, k)
     with scope("arrive2"):
         arrive((2, 0))
     with scope("moved_back"):
@@ -620,30 +612,32 @@
         fill_edges(3)
     with scope("wait1"):
         all_out(1).wait_recv()
+    with scope("arrive2"):
+        arrive(*[(2, c) for c in range(1, pairs)], *[(3, c) for c in range(pairs - 1)])
     with scope("pack1"):
+        extra_in[0:levels, :] = gather_extra()
         for p in range(block_pairs):
             pack(1, p)
-        extra_in[0:levels, :] = gather_spare(1, pick_extra)
-        extra_out[...] = jnp.zeros_like(extra_out)
-    with scope("extra"):
-        solve_extra([(t, j) for t in range(2) for j in range(pairs)])
-    with scope("late2a"):
-        deal(1, [0], [solve(1, 0)], True)
-        solve_extra([(2, 0)])
-    with scope("arrive2b"):
-        arrive(*[(2, c) for c in range(1, pairs)])
-    with scope("late2b"):
-        late(list(range(1, pairs)))
+    with scope("late"):
+        answers = [solve(1, p) for p in range(block_pairs - 1)]
+        steps = [(t, j) for t in range(Z) for j in range(pairs)]
+        extra = jnp.zeros(extra_in.shape, jnp.bfloat16)
+        extra = solve_extra(extra, steps[:-1])
     with scope("arrive3"):
-        arrive(*[(3, c) for c in range(pairs - 1)])
-    with scope("late3a"):
-        late(list(range(pairs, block_pairs - 1)))
-    with scope("arrive3b"):
         arrive((3, pairs - 1))
-    with scope("late3b"):
-        late([block_pairs - 1])
-        scatter_spare(1, extra_out[...], pick_extra, is_extra)
-        start_back(1)
+    with scope("last"):
+        extra = solve_extra(extra, steps[-1:])
+        answers.append(solve(1, block_pairs - 1))
+        extra_back = jnp.dot(
+            extra, put_extra[...], preferred_element_type=jnp.float32
+        ).astype(jnp.bfloat16)
+        for k in range(W - 1, -1, -1):
+            block = deal(answers, k)
+            solved[1, k] = jnp.where(
+                is_extra(k), extra_back[:, k * LANES : (k + 1) * LANES], block
+            )
+            if k > 0:
+                back_copy(1, k).start()
 
     fetches[6].wait()
     fetches[7].wait()
@@ -680,9 +674,22 @@
             lax.fori_loop(0, W // 2 - 1, step, 0)
         with scope(f"back{b}_0"):
             some_back(b, 1, 1).wait_recv()
-            collect(b, 0, solved[b, 0], returned[b, 1])
+            if b == 0:
+                collect(b, 0, solved[b, 0], returned[b, 1])
+            else:
+                total[...] += jnp.dot(
+                    jnp.concatenate([solved[b, 0], returned[b, 1]], axis=1),
+                    last_pick[...],
+                    preferred_element_type=jnp.float32,
+                )
 
     gather_back(0)
+    with scope("last_pick"):
+        targets = jnp.concatenate([target_of(1, 0), target_of(1, 1)], axis=1)
+        targets = jnp.broadcast_to(targets.astype(jnp.float32), (TABLE_ROWS, 2 * LANES))
+        targets = targets.T[:, 0:1].astype(jnp.int32)
+        at = lax.broadcasted_iota(jnp.int32, (2 * LANES, width), 1)
+        last_pick[...] = jnp.where(at == targets, 1.0, 0.0).astype(jnp.bfloat16)
     gather_back(1)
 
     with scope("final"):
@@ -788,7 +795,8 @@
             pltpu.VMEM((ceil_to(2 * pairs, TABLE_ROWS), tiles * LANES), jnp.int32),
             pltpu.VMEM((W * LANES, extra_width), jnp.bfloat16),
             pltpu.VMEM((rows, extra_width), jnp.bfloat16),
-            pltpu.VMEM((rows, extra_width), jnp.bfloat16),
+            pltpu.VMEM((extra_width, W * LANES), jnp.bfloat16),
+            pltpu.VMEM((2 * LANES, width), jnp.bfloat16),
             pltpu.VMEM((rows, width), jnp.float32),
             pltpu.SemaphoreType.DMA,
             pltpu.SemaphoreType.DMA((Z,)),
@@ -803,7 +811,7 @@
             pltpu.SemaphoreType.DMA((8,)),
         ],
         compiler_params=pltpu.CompilerParams(
-            collective_id=0, has_side_effects=True, vmem_limit_bytes=52 * 1024 * 1024
+            collective_id=0, has_side_effects=True, vmem_limit_bytes=58 * 1024 * 1024
         ),
     )(
         *[

time: 30.7 us -> 30.5 us (level)
  no operation moved by 1% of the time
where the time goes in v6:
time: 30.5 us; the launch traced here: 30.3 us
  Pallas kernels  29.3 us (96%)
  local copies, waits for them, and re-layouts  1 us (3%)
    pallas_call x1, Pallas kernels, shards(): pl.pallas_call(functools.partial(kernel, (Z, W, levels, slots, pairs)), o...  29.3 us
    unnamed x1, local copies, waits for them, and re-layouts  1 us

profile of v6, /device:TPU:0, one launch (start us, length us, event | category | flops | bytes accessed | tf_op | source)
XLA Modules:
  0.0 30.3 jit_solution(6215403909181025770)
XLA Ops:
  0.0 29.3 %shard_map.82 = bf16[275,1930]{1,0:T(8,128)(2,1)S(1)} custom-call(s32[5]{0:T(128)} %held_far.1, s32[3]{0:T(128)} %lows_far.1, bf16[275,1930]{1,0:T(8,128)(2,1)} %state_far.1, bf16[3,137,2,137]{3,2,1,0:T(2,128)(2,1)} %bitcast.1, bf16[137,137]{1,0:T(8,128)(2,1)} %height_far.1, bf16[137]{0:T(256)(128)(2,1)} %pressure_far.1, bf16[137,137]{1,0:T(8,128)(2,1)} %thermal_far.1, ...), custom_call_target="tpu_custom_call" | custom-call | tf_op jit(solution)/shard_map/pallas_call | solution.py:769
  29.3 1.0 %copy.10 = bf16[275,1930]{1,0:T(8,128)(2,1)} copy(bf16[275,1930]{1,0:T(8,128)(2,1)S(1)} %shard_map.82) | data formatting | bytes 2123000

commit v7 on v6

--- a/solution.py
+++ b/solution.py
@@ -11,7 +11,6 @@
 LANES = 128
 ROWS_TILE = 16
 TABLE_ROWS = 8
-NEAR_ROWS = 16
 CHUNK = 256
 KEEP_BYTES = 24 << 20
 scope = jax.named_scope
@@ -69,19 +68,24 @@
     back_send,
     back_recv,
     fetch_sem,
+    known,
 ):
     Z, W, levels, slots, pairs = size
     half_count = Z * W * pairs
     truncation = 2 * half_count - 1
     slot_width = 2 * (truncation + 2)
     width = slots * slot_width
+    rows = solved.shape[2]
     denom = float(truncation * (truncation + 1))
     per_pair = 4 * slots
     block_pairs = 2 * pairs
     first_extra = block_pairs * per_pair
-    moved = per_pair - 2
+    fold = rows - levels
+    spans = -(-levels // fold)
     tiles = packed.shape[2] // LANES
     last_slot = slots - 1
+    stages = W.bit_length() - 1
+    rounds = max(stages, Z - 1)
     tail = levels - LANES
     border = 2 * pairs * tail
     keep = pick.shape[1] > 1
@@ -98,9 +102,25 @@
             other = other + (1 << i) * (mine + flip - 2 * mine * flip)
         return other
 
-    def greet(k, carry):
-        pl.semaphore_signal(barrier, inc=1, device_id=(z, peer(k)), device_id_type=MESH)
-        return carry
+    def tell(semaphore):
+        for i in range(stages):
+            pl.semaphore_signal(
+                semaphore, inc=1, device_id=(z, peer(1 << i)), device_id_type=MESH
+            )
+
+        @pl.when(z > 0)
+        def _():
+            pl.semaphore_signal(
+                semaphore, inc=1, device_id=(lax.rem(z + Z - 1, Z), w), device_id_type=MESH
+            )
+
+        @pl.when(z < Z - 1)
+        def _():
+            pl.semaphore_signal(
+                semaphore, inc=1, device_id=(lax.rem(z + 1, Z), w), device_id_type=MESH
+            )
+
+    near_count = stages + jnp.where(z > 0, 1, 0) + jnp.where(z < Z - 1, 1, 0)
 
     fetches = [
         pltpu.make_async_copy(far, near, fetch_sem.at[i])
@@ -117,12 +137,8 @@
             ]
         )
     ]
-    for k in range(1, Z):
-        pl.semaphore_signal(barrier, inc=1, device_id=(lax.rem(z + k, Z), w), device_id_type=MESH)
-    for fetch in fetches[:3]:
-        fetch.start()
-    lax.fori_loop(1, W, greet, 0)
-    for fetch in fetches[3:]:
+    tell(barrier)
+    for fetch in fetches:
         fetch.start()
 
     lane = lax.broadcasted_iota(jnp.int32, (1, LANES), 1)
@@ -142,8 +158,6 @@
     for j in range(pairs):
         low_tile = jnp.where(table_row == j, lows[j], low_tile)
     low_rows[z] = low_tile
-
-    rows = matrices.shape[2]
 
     def split_inverses():
         fetches[2].wait()
@@ -177,7 +191,7 @@
             split_inverses()
 
     with scope("barrier"):
-        pl.semaphore_wait(barrier, W + Z - 2)
+        pl.semaphore_wait(barrier, near_count)
 
     def z_copy(g, c, way):
         if c < pairs:
@@ -283,16 +297,51 @@
             device_id_type=MESH,
         )
 
-    for distance in range(1, Z):
-        send_rows(distance)
+    send_rows(1)
+    tell(known.at[0])
 
     @pl.when(z == Z - 1)
     def _():
         with scope("split_end"):
             split_inverses()
 
-    for c in [pairs, *range(pairs)]:
-        forward(z, c)
+    own_chunks = [pairs, *range(pairs)]
+
+    def steps(t, first, stop=None):
+        return [(t, c) for c in own_chunks[first:stop]]
+
+    to_right = jnp.logical_and(z > 0, 2 * z >= Z)
+    to_left = jnp.logical_and(z < Z - 1, 2 * z < Z)
+    free_right = jnp.logical_and(to_right, z < Z - 1)
+    free_left = jnp.logical_and(to_left, z > 0)
+
+    def send_middle():
+        @pl.when(middle)
+        def _():
+            for c in own_chunks[1:]:
+                send_own(c, False)
+
+    def send_ends():
+        @pl.when(jnp.logical_not(middle))
+        def _():
+            for c in own_chunks[1:]:
+                send_own(c, False)
+
+    def send_own(c, free):
+        right = free_right if free else jnp.logical_not(free_right)
+        left = free_left if free else jnp.logical_not(free_left)
+
+        @pl.when(jnp.logical_and(right, z < Z - 1))
+        def _():
+            z_copy(z, c, 0).start()
+
+        @pl.when(jnp.logical_and(left, z > 0))
+        def _():
+            z_copy(z, c, 1).start()
+
+    send_own(pairs, False)
+    for c in own_chunks:
+        send_own(c, True)
 
     column = lax.broadcasted_iota(jnp.int32, (1, width), 1)
     column_order = jnp.full((1, width), -1, jnp.int32)
@@ -306,15 +355,18 @@
         for ref, dimension in ((pick_extra, 0), (put_extra, 1)):
             row = lax.broadcasted_iota(jnp.int32, ref.shape, dimension)
             at = lax.broadcasted_iota(jnp.int32, ref.shape, 1 - dimension)
-            k, own = row // LANES, lax.rem(row, LANES)
-            start = per_pair * lax.rem(k, block_pairs) + moved
-            hole = jnp.logical_and(own >= start, own < start + 2)
-            last = 2 * last_slot + own - start
-            wanted = 2 * slots * k + jnp.where(hole, last, own - first_extra)
-            valid = jnp.logical_or(hole, own >= first_extra)
-            ref[...] = jnp.where(jnp.logical_and(valid, at == wanted), 1.0, 0.0).astype(
-                jnp.bfloat16
-            )
+            k, own = lax.rem(row // LANES, W), lax.rem(row, LANES)
+            first_half = row < W * LANES
+            if dimension == 0:
+                last = own - first_extra
+                valid = jnp.logical_or(first_half, own < first_extra + 2)
+                valid = jnp.logical_and(valid, own >= first_extra)
+            else:
+                last = own // spans
+                valid = jnp.where(first_half, own - first_extra, 2 * spans - 1 - own) >= 0
+            offset = jnp.where(first_half, own - first_extra, 2 * last_slot + last)
+            wanted = jnp.where(valid, 2 * slots * k + offset, -1)
+            ref[...] = jnp.where(at == wanted, 1.0, 0.0).astype(jnp.bfloat16)
 
     def drive_right():
         coefficient = (column - column_start) // 2
@@ -342,33 +394,44 @@
             state[0:levels, :].astype(jnp.float32) + lap_scale * drive
         ).astype(jnp.bfloat16)
 
+    for i in range(1, rounds):
+        with scope(f"known{i}"):
+            pl.semaphore_wait(known.at[i - 1], near_count)
+        if i + 1 < Z:
+            send_rows(i + 1)
+        if i + 1 < rounds:
+            tell(known.at[i])
+        if i == 1:
+            send_middle()
+    send_ends()
     with scope("drive"):
         drive_right()
     choose()
     with scope("rows_wait"):
-        for t in range(1, 3):
-            wait_row(groups[t])
-    table = [low_rows[groups[t]][0:pairs] for t in range(3)]
-    table += [jnp.broadcast_to(orders, (NEAR_ROWS - 3 * pairs, LANES))]
+        wait_row(groups[1])
+    table = [low_rows[groups[t]][0:pairs] for t in range(2)]
+    table += [jnp.broadcast_to(orders, (TABLE_ROWS - 2 * pairs, LANES))]
     info[w] = jnp.concatenate(table, axis=0)
     send_table(info, 0)
     with scope("row_far"):
+        wait_row(groups[2])
         wait_row(groups[3])
-    far_info[w] = low_rows[groups[3]]
+    table = [low_rows[groups[t]][0:pairs] for t in range(2, 4)]
+    table += [jnp.zeros((TABLE_ROWS - 2 * pairs, LANES), jnp.int32)]
+    far_info[w] = jnp.concatenate(table, axis=0)
     send_table(far_info, 1)
 
     @pl.when(middle)
     def _():
         with scope("relay_a"):
-            relay_now((1, pairs), (1, 0), (2, pairs), (2, 0), (1, 1))
+            relay_now(*steps(1, 0, 2), *steps(2, 0, 2), *steps(1, 2, 3))
 
     with scope("info_wait"):
         all_tables(info, 0).wait_recv()
 
     def low_of(d, t, j):
-        if t < 3:
-            return info[d][t * pairs + j : t * pairs + j + 1]
-        return far_info[d][j : j + 1]
+        row = t % 2 * pairs + j
+        return (info if t < 2 else far_info)[d][row : row + 1]
 
     def target_of(b, k):
         d = peer(k)
@@ -376,30 +439,27 @@
         low = jnp.zeros((1, LANES), jnp.int32)
         for p in range(block_pairs):
             low = jnp.where(pair == p, low_of(d, 2 * b + p // pairs, p % pairs), low)
-        slot, member, order = lane_slot, lane_member, orders
+        slot, order = lane_slot, orders
+        used = lane >= 0
         if b == 0:
-            low = jnp.where(spare, low_of(d, 2, 0), low)
             slot = jnp.where(spare, last_slot, slot)
-            member = jnp.where(spare, 1, member)
             order = jnp.where(spare, held[last_slot], order)
+            used = lane < first_extra + 2
         merged = jnp.where(order <= low, low - order, truncation + 1 - low)
-        position = jnp.where(member == 0, merged, truncation - low - order)
-        used = order >= 0
-        if b == 0:
-            used = jnp.logical_and(used, lane < first_extra + 2)
-        else:
-            hole = jnp.logical_and(pair == 0, lax.rem(lane, per_pair) >= moved)
-            extra = jnp.logical_or(spare, hole)
-            position = jnp.where(extra, truncation + 1 - order, position)
+        position = jnp.where(lane_member == 0, merged, truncation - low - order)
+        position = jnp.where(spare, truncation + 1 - order, position)
         target = slot * slot_width + 2 * position + lane_part
-        return jnp.where(used, target, -1)
+        return jnp.where(jnp.logical_and(used, order >= 0), target, -1)
 
     def build(b, i, place):
         at = lax.broadcasted_iota(jnp.int32, (width, LANES), 0)
         for h in range(2):
-            pick[b, place, :, h * LANES : (h + 1) * LANES] = jnp.where(
+            pick[block_of(b), place, :, h * LANES : (h + 1) * LANES] = jnp.where(
                 at == target_of(b, 2 * i + h), 1.0, 0.0
             ).astype(jnp.bfloat16)
+
+    def block_of(b):
+        return b if keep else 0
 
     def place_of(i):
         return i if keep else 0
@@ -433,7 +493,7 @@
                 count = min(CHUNK, width - start)
                 at = lax.broadcasted_iota(jnp.int32, (count, 2 * LANES), 0) + start
                 chosen = jnp.where(at == targets, 1.0, 0.0).astype(jnp.bfloat16)
-                pick[b, place_of(i), start : start + count, :] = chosen
+                pick[block_of(b), place_of(i), start : start + count, :] = chosen
                 message += jnp.dot(
                     right[:, start : start + count], chosen, preferred_element_type=jnp.float32
                 )
@@ -474,21 +534,21 @@
     with scope("send0"):
         send_block(0, 0, W // 4)
     with scope("relay_b"):
-        relay((1, 2), (2, 1))
+        relay(*steps(1, 3), *steps(2, 2, 3))
     with scope("send0b"):
         send_block(0, W // 4, W // 2)
     with scope("relay_c"):
-        relay((2, 2), (3, pairs))
+        relay(*steps(2, 3), *steps(3, 0, 1))
     with scope("far_wait"):
         all_tables(far_info, 1).wait_recv()
     with scope("send1"):
         send_block(1, 0, W // 4)
     with scope("relay_d"):
-        relay((3, 0))
+        relay(*steps(3, 1, 2))
     with scope("send1b"):
         send_block(1, W // 4, W // 2)
     with scope("relay_e"):
-        relay((3, 1))
+        relay(*steps(3, 2, 3))
     for b in range(2):
         arrived[b, 0] = outgoing[b, 0]
 
@@ -510,7 +570,7 @@
         return jnp.concatenate([row] * tiles, axis=1)
 
     source_orders = [
-        info[peer(k)][3 * pairs : 3 * pairs + 1] for k in range(W)
+        info[peer(k)][2 * pairs : 2 * pairs + 1] for k in range(W)
     ]
 
     def place(p, k):
@@ -551,15 +611,22 @@
             block = jnp.where(place(p, k), answers[p][:, part], block)
         return block
 
-    def gather_extra():
-        columns = jnp.concatenate([arrived[1, k, 0:levels, :] for k in range(W)], axis=1)
-        return jnp.dot(columns, pick_extra[...], preferred_element_type=jnp.float32).astype(
-            jnp.bfloat16
-        )
-
-    def is_extra(k):
-        start = per_pair * (k % block_pairs) + moved
-        return jnp.logical_or(spare, jnp.logical_and(lane >= start, lane < start + 2))
+    def gather_extra(b):
+        columns = jnp.concatenate([arrived[b, k, 0:levels, :] for k in range(W)], axis=1)
+        start = (1 - b) * W * LANES
+        chosen = pick_extra[start : start + W * LANES, :]
+        return jnp.dot(columns, chosen, preferred_element_type=jnp.float32)
+
+    def fold_mask(shape):
+        level = lax.broadcasted_iota(jnp.int32, shape, 0)
+        own = lax.rem(lax.broadcasted_iota(jnp.int32, shape, 1), LANES)
+        return jnp.logical_and(level // fold == lax.rem(own, spans), own < 2 * spans)
+
+    def fold_rows(shape, dimension):
+        level = lax.broadcasted_iota(jnp.int32, shape, 1 - dimension)
+        at = lax.broadcasted_iota(jnp.int32, shape, dimension)
+        inside = jnp.logical_and(level < levels, at - tail == lax.rem(level, fold))
+        return jnp.where(inside, 1.0, 0.0).astype(jnp.bfloat16)
 
     extra_width = extra_in.shape[1]
 
@@ -583,7 +650,7 @@
         return y
 
     with scope("arrive1"):
-        relay((3, 2))
+        relay(*steps(3, 3))
         arrive((1, pairs), *[(1, c) for c in range(pairs)], (2, pairs))
     fill_edges(1)
     fill_edges(2)
@@ -594,48 +661,50 @@
             pack(0, p)
     with scope("near"):
         answers = [solve(0, p) for p in range(block_pairs)]
-        for k in range(W):
-            solved[0, k] = deal(answers, k)
-    with scope("arrive2"):
-        arrive((2, 0))
-    with scope("moved_back"):
-        for k in range(W - 2, -1, -2):
-            x = [arrived[0, k + h, 0:levels, :] for h in range(2)]
-            y = times(2, 0, 1, jnp.concatenate(x, axis=1)).astype(jnp.bfloat16)
-            for h in range(2):
-                part = y[:, h * LANES : (h + 1) * LANES]
-                solved[0, k + h] = jnp.where(spare, part, solved[0, k + h])
-                if k + h > 0:
-                    back_copy(0, k + h).start()
+        for k in range(W - 1, -1, -1):
+            solved[0, k] = jnp.where(spare, jnp.zeros((), jnp.bfloat16), deal(answers, k))
+            if k > 0:
+                back_copy(0, k).start()
+    with scope("extra0"):
+        extra_part = gather_extra(0)
     with scope("edges3"):
         arrive((3, pairs))
         fill_edges(3)
     with scope("wait1"):
         all_out(1).wait_recv()
     with scope("arrive2"):
-        arrive(*[(2, c) for c in range(1, pairs)], *[(3, c) for c in range(pairs - 1)])
+        arrive(*[(2, c) for c in range(pairs)], *[(3, c) for c in range(pairs - 1)])
     with scope("pack1"):
-        extra_in[0:levels, :] = gather_extra()
+        extra_in[0:levels, :] = (gather_extra(1) + extra_part).astype(jnp.bfloat16)
         for p in range(block_pairs):
             pack(1, p)
     with scope("late"):
         answers = [solve(1, p) for p in range(block_pairs - 1)]
-        steps = [(t, j) for t in range(Z) for j in range(pairs)]
+        order = [(t, j) for t in range(Z) for j in range(pairs)]
         extra = jnp.zeros(extra_in.shape, jnp.bfloat16)
-        extra = solve_extra(extra, steps[:-1])
+        extra = solve_extra(extra, order[:-1])
     with scope("arrive3"):
         arrive((3, pairs - 1))
     with scope("last"):
-        extra = solve_extra(extra, steps[-1:])
+        extra = solve_extra(extra, order[-1:])
         answers.append(solve(1, block_pairs - 1))
-        extra_back = jnp.dot(
-            extra, put_extra[...], preferred_element_type=jnp.float32
-        ).astype(jnp.bfloat16)
+        extra_back = jnp.dot(extra, put_extra[...], preferred_element_type=jnp.float32)
+        half = W * LANES
+        spread_last = jnp.where(fold_mask((rows, half)), extra_back[:, half:], 0.0)
+        folded = jnp.dot(
+            fold_rows((rows - LANES, rows), 0),
+            spread_last.astype(jnp.bfloat16),
+            preferred_element_type=jnp.float32,
+        )
+        under = lax.broadcasted_iota(jnp.int32, (rows - LANES, LANES), 0) >= tail
+        here = jnp.logical_and(under, lane < 2 * spans)
         for k in range(W - 1, -1, -1):
+            part = slice(k * LANES, (k + 1) * LANES)
             block = deal(answers, k)
-            solved[1, k] = jnp.where(
-                is_extra(k), extra_back[:, k * LANES : (k + 1) * LANES], block
-            )
+            block = jnp.where(spare, extra_back[:, part].astype(jnp.bfloat16), block)
+            bottom = jnp.where(here, folded[:, part], block[LANES:].astype(jnp.float32))
+            solved[1, k, 0:LANES, :] = block[0:LANES]
+            solved[1, k, LANES:rows, :] = bottom.astype(jnp.bfloat16)
             if k > 0:
                 back_copy(1, k).start()
 
@@ -658,37 +727,57 @@
             build(b, i, 0)
         total[...] += lax.dot_general(
             jnp.concatenate([first, second], axis=1),
-            pick[b, place_of(i)],
+            pick[block_of(b), place_of(i)],
             (((1,), (1,)), ((), ())),
             preferred_element_type=jnp.float32,
         )
 
     def gather_back(b):
-        def step(n, carry):
-            i = W // 2 - 1 - n
+        last_pair = W // 2 - 1
+        with scope(f"back{b}_0"):
+            some_back(b, 1, 1).wait_recv()
+            collect(b, 0, solved[b, 0], returned[b, 1])
+
+        def step(i, carry):
             some_back(b, 2 * i, 2).wait_recv()
             collect(b, i, returned[b, 2 * i], returned[b, 2 * i + 1])
             return carry
 
         with scope(f"back{b}"):
-            lax.fori_loop(0, W // 2 - 1, step, 0)
-        with scope(f"back{b}_0"):
-            some_back(b, 1, 1).wait_recv()
+            lax.fori_loop(1, last_pair, step, 0)
+        with scope(f"back{b}_wait"):
+            some_back(b, W - 2, 2).wait_recv()
+        with scope(f"back{b}_last"):
             if b == 0:
-                collect(b, 0, solved[b, 0], returned[b, 1])
+                collect(b, last_pair, returned[b, W - 2], returned[b, W - 1])
             else:
+                bottom = solved[b, 0, LANES:rows, :].astype(jnp.float32)
+                for k in range(1, W):
+                    bottom = bottom + returned[b, k, LANES:rows, :].astype(jnp.float32)
+                unfolded = jnp.dot(
+                    fold_rows((rows, rows - LANES), 1),
+                    bottom.astype(jnp.bfloat16),
+                    preferred_element_type=jnp.float32,
+                )
+                unfolded = jnp.where(fold_mask((rows, LANES)), unfolded, 0.0)
                 total[...] += jnp.dot(
-                    jnp.concatenate([solved[b, 0], returned[b, 1]], axis=1),
+                    jnp.concatenate(
+                        [returned[b, W - 2], returned[b, W - 1], unfolded.astype(jnp.bfloat16)],
+                        axis=1,
+                    ),
                     last_pick[...],
                     preferred_element_type=jnp.float32,
                 )
 
     gather_back(0)
     with scope("last_pick"):
-        targets = jnp.concatenate([target_of(1, 0), target_of(1, 1)], axis=1)
-        targets = jnp.broadcast_to(targets.astype(jnp.float32), (TABLE_ROWS, 2 * LANES))
+        order = held[last_slot]
+        folded_to = last_slot * slot_width + 2 * (truncation + 1 - order) + lane // spans
+        folded_to = jnp.where(jnp.logical_and(order >= 0, lane < 2 * spans), folded_to, -1)
+        targets = jnp.concatenate([target_of(1, W - 2), target_of(1, W - 1), folded_to], axis=1)
+        targets = jnp.broadcast_to(targets.astype(jnp.float32), (TABLE_ROWS, 3 * LANES))
         targets = targets.T[:, 0:1].astype(jnp.int32)
-        at = lax.broadcasted_iota(jnp.int32, (2 * LANES, width), 1)
+        at = lax.broadcasted_iota(jnp.int32, (3 * LANES, width), 1)
         last_pick[...] = jnp.where(at == targets, 1.0, 0.0).astype(jnp.bfloat16)
     gather_back(1)
 
@@ -781,22 +870,22 @@
             pltpu.VMEM(thermal_response_matrix.shape, jnp.bfloat16),
             pltpu.VMEM(mass_row.shape, jnp.bfloat16),
             pltpu.VMEM((Z, TABLE_ROWS, LANES), jnp.int32),
-            pltpu.VMEM((W, NEAR_ROWS, LANES), jnp.int32),
+            pltpu.VMEM((W, TABLE_ROWS, LANES), jnp.int32),
             pltpu.VMEM((W, TABLE_ROWS, LANES), jnp.int32),
             pltpu.VMEM((Z, 2 * pairs, rows, levels), jnp.bfloat16),
             pltpu.VMEM((Z, LANES, LANES), jnp.bfloat16),
             pltpu.VMEM((rows, width), jnp.bfloat16),
-            pltpu.VMEM((2, places, width, 2 * LANES), jnp.bfloat16),
+            pltpu.VMEM((2 if places > 1 else 1, places, width, 2 * LANES), jnp.bfloat16),
             block,
             block,
             block,
             block,
             pltpu.VMEM((4 * pairs, rows, tiles * LANES), jnp.bfloat16),
             pltpu.VMEM((ceil_to(2 * pairs, TABLE_ROWS), tiles * LANES), jnp.int32),
-            pltpu.VMEM((W * LANES, extra_width), jnp.bfloat16),
+            pltpu.VMEM((2 * W * LANES, extra_width), jnp.bfloat16),
             pltpu.VMEM((rows, extra_width), jnp.bfloat16),
-            pltpu.VMEM((extra_width, W * LANES), jnp.bfloat16),
-            pltpu.VMEM((2 * LANES, width), jnp.bfloat16),
+            pltpu.VMEM((extra_width, 2 * W * LANES), jnp.bfloat16),
+            pltpu.VMEM((3 * LANES, width), jnp.bfloat16),
             pltpu.VMEM((rows, width), jnp.float32),
             pltpu.SemaphoreType.DMA,
             pltpu.SemaphoreType.DMA((Z,)),
@@ -809,9 +898,10 @@
             pltpu.SemaphoreType.DMA((2,)),
             pltpu.SemaphoreType.DMA((2, W // 2)),
             pltpu.SemaphoreType.DMA((8,)),
+            pltpu.SemaphoreType.REGULAR((max(W.bit_length() - 2, Z - 2),)),
         ],
         compiler_params=pltpu.CompilerParams(
-            collective_id=0, has_side_effects=True, vmem_limit_bytes=58 * 1024 * 1024
+            collective_id=0, has_side_effects=True, vmem_limit_bytes=61000 * 1024
         ),
     )(
         *[

time: 30.5 us -> 29.8 us (0.977)
  Pallas kernels: 29.3 us -> 28.7 us
    pallas_call x1, Pallas kernels: 29.3 us -> 28.7 us  [shards(): pl.pallas_call(functools.partial(kernel, (Z, W, levels, slots, pairs)), o...]
where the time goes in v7:
time: 29.8 us; the launch traced here: 29.7 us
  Pallas kernels  28.7 us (96%)
  local copies, waits for them, and re-layouts  1 us (3%)
    pallas_call x1, Pallas kernels, shards(): pl.pallas_call(functools.partial(kernel, (Z, W, levels, slots, pairs)), o...  28.7 us
    unnamed x1, local copies, waits for them, and re-layouts  1 us

profile of v7, /device:TPU:0, one launch (start us, length us, event | category | flops | bytes accessed | tf_op | source)
XLA Modules:
  0.0 29.7 jit_solution(3971890094589603551)
XLA Ops:
  0.0 28.7 %shard_map.82 = bf16[275,1930]{1,0:T(8,128)(2,1)S(1)} custom-call(s32[5]{0:T(128)} %held_far.1, s32[3]{0:T(128)} %lows_far.1, bf16[275,1930]{1,0:T(8,128)(2,1)} %state_far.1, bf16[3,137,2,137]{3,2,1,0:T(2,128)(2,1)} %bitcast.1, bf16[137,137]{1,0:T(8,128)(2,1)} %height_far.1, bf16[137]{0:T(256)(128)(2,1)} %pressure_far.1, bf16[137,137]{1,0:T(8,128)(2,1)} %thermal_far.1, ...), custom_call_target="tpu_custom_call" | custom-call | tf_op jit(solution)/shard_map/pallas_call | solution.py:858
  28.7 1.0 %copy.10 = bf16[275,1930]{1,0:T(8,128)(2,1)} copy(bf16[275,1930]{1,0:T(8,128)(2,1)S(1)} %shard_map.82) | data formatting | bytes 2123000

commit v8 on v7

--- a/solution.py
+++ b/solution.py
@@ -138,6 +138,14 @@
         )
     ]
     tell(barrier)
+    for distance in range(2, Z):
+
+        @pl.when(z + distance < Z)
+        def _():
+            pl.semaphore_signal(
+                barrier, inc=1, device_id=(lax.rem(z + distance, Z), w), device_id_type=MESH
+            )
+
     for fetch in fetches:
         fetch.start()
 
@@ -191,7 +199,7 @@
             split_inverses()
 
     with scope("barrier"):
-        pl.semaphore_wait(barrier, near_count)
+        pl.semaphore_wait(barrier, near_count + jnp.where(z > 1, z - 1, 0))
 
     def z_copy(g, c, way):
         if c < pairs:
@@ -253,8 +261,8 @@
             device_id_type=MESH,
         )
 
-    def send_rows(distance):
-        for step in (-distance, distance):
+    def send_rows(*distances):
+        for step in distances:
 
             @pl.when(jnp.logical_and(z + step >= 0, z + step < Z))
             def _():
@@ -297,7 +305,7 @@
             device_id_type=MESH,
         )
 
-    send_rows(1)
+    send_rows(-1, 1, *range(-2, -Z, -1))
     tell(known.at[0])
 
     @pl.when(z == Z - 1)
@@ -404,15 +412,15 @@
         if i == 1:
             send_middle()
     send_ends()
-    with scope("drive"):
-        drive_right()
-    choose()
     with scope("rows_wait"):
         wait_row(groups[1])
     table = [low_rows[groups[t]][0:pairs] for t in range(2)]
     table += [jnp.broadcast_to(orders, (TABLE_ROWS - 2 * pairs, LANES))]
     info[w] = jnp.concatenate(table, axis=0)
     send_table(info, 0)
+    with scope("drive"):
+        drive_right()
+    choose()
     with scope("row_far"):
         wait_row(groups[2])
         wait_row(groups[3])
@@ -424,7 +432,7 @@
     @pl.when(middle)
     def _():
         with scope("relay_a"):
-            relay_now(*steps(1, 0, 2), *steps(2, 0, 2), *steps(1, 2, 3))
+            relay_now(*steps(1, 0, 3), *steps(2, 0, 2))
 
     with scope("info_wait"):
         all_tables(info, 0).wait_recv()

time: 29.8 us -> 28.9 us (0.970)
  Pallas kernels: 28.7 us -> 27.8 us
    pallas_call x1, Pallas kernels: 28.7 us -> 27.8 us  [shards(): pl.pallas_call(functools.partial(kernel, (Z, W, levels, slots, pairs)), o...]
where the time goes in v8:
time: 28.9 us; the launch traced here: 28.8 us
  Pallas kernels  27.8 us (96%)
  local copies, waits for them, and re-layouts  1 us (3%)
    pallas_call x1, Pallas kernels, shards(): pl.pallas_call(functools.partial(kernel, (Z, W, levels, slots, pairs)), o...  27.8 us
    unnamed x1, local copies, waits for them, and re-layouts  1 us

profile of v8, /device:TPU:0, one launch (start us, length us, event | category | flops | bytes accessed | tf_op | source)
XLA Modules:
  0.0 28.8 jit_solution(7575323279765413277)
XLA Ops:
  0.0 27.8 %shard_map.82 = bf16[275,1930]{1,0:T(8,128)(2,1)S(1)} custom-call(s32[5]{0:T(128)} %held_far.1, s32[3]{0:T(128)} %lows_far.1, bf16[275,1930]{1,0:T(8,128)(2,1)} %state_far.1, bf16[3,137,2,137]{3,2,1,0:T(2,128)(2,1)} %bitcast.1, bf16[137,137]{1,0:T(8,128)(2,1)} %height_far.1, bf16[137]{0:T(256)(128)(2,1)} %pressure_far.1, bf16[137,137]{1,0:T(8,128)(2,1)} %thermal_far.1, ...), custom_call_target="tpu_custom_call" | custom-call | tf_op jit(solution)/shard_map/pallas_call | solution.py:866
  27.8 1.0 %copy.10 = bf16[275,1930]{1,0:T(8,128)(2,1)} copy(bf16[275,1930]{1,0:T(8,128)(2,1)S(1)} %shard_map.82) | data formatting | bytes 2123000

commit v9 on v8

--- a/solution.py
+++ b/solution.py
@@ -318,10 +318,8 @@
     def steps(t, first, stop=None):
         return [(t, c) for c in own_chunks[first:stop]]
 
-    to_right = jnp.logical_and(z > 0, 2 * z >= Z)
-    to_left = jnp.logical_and(z < Z - 1, 2 * z < Z)
-    free_right = jnp.logical_and(to_right, z < Z - 1)
-    free_left = jnp.logical_and(to_left, z > 0)
+    free_right = z == Z - 2
+    free_left = z > 0
 
     def send_middle():
         @pl.when(middle)

time: 28.9 us -> 28.9 us (level)
  no operation moved by 1% of the time
where the time goes in v9:
time: 28.9 us; the launch traced here: 28.8 us
  Pallas kernels  27.8 us (96%)
  local copies, waits for them, and re-layouts  1 us (3%)
    pallas_call x1, Pallas kernels, shards(): pl.pallas_call(functools.partial(kernel, (Z, W, levels, slots, pairs)), o...  27.8 us
    unnamed x1, local copies, waits for them, and re-layouts  1 us

profile of v9, /device:TPU:0, one launch (start us, length us, event | category | flops | bytes accessed | tf_op | source)
XLA Modules:
  0.0 28.8 jit_solution(11597366498046302467)
XLA Ops:
  0.0 27.8 %shard_map.82 = bf16[275,1930]{1,0:T(8,128)(2,1)S(1)} custom-call(s32[5]{0:T(128)} %held_far.1, s32[3]{0:T(128)} %lows_far.1, bf16[275,1930]{1,0:T(8,128)(2,1)} %state_far.1, bf16[3,137,2,137]{3,2,1,0:T(2,128)(2,1)} %bitcast.1, bf16[137,137]{1,0:T(8,128)(2,1)} %height_far.1, bf16[137]{0:T(256)(128)(2,1)} %pressure_far.1, bf16[137,137]{1,0:T(8,128)(2,1)} %thermal_far.1, ...), custom_call_target="tpu_custom_call" | custom-call | tf_op jit(solution)/shard_map/pallas_call | solution.py:864
  27.8 1.0 %copy.10 = bf16[275,1930]{1,0:T(8,128)(2,1)} copy(bf16[275,1930]{1,0:T(8,128)(2,1)S(1)} %shard_map.82) | data formatting | bytes 2123000
